TPU v7x, 64 devices: a 2x2x8 block of a 4x4x8 slice. The times are simulated.
64 devices in a mesh: dp: 4 (over x, y), sp: 16 (over z, core).
Axes of the slice: x: 2, y: 2, z: 8, core: 2. Of those that a mesh axis runs over, the one named last changes fastest.
The devices are a block of a 4x4x8 slice.
Arguments:
- tokens: bfloat16 [65536, 1536], P(('dp', 'sp')), parts along dimension 0
- w_q: bfloat16 [1536, 1536], replicated
- w_k: bfloat16 [1536, 1536], replicated
- w_v: bfloat16 [1536, 1536], replicated
- w_o: bfloat16 [1536, 1536], replicated
- grad_y: bfloat16 [65536, 1536], P(('dp', 'sp')), parts along dimension 0
Outputs:
- output 1: bfloat16 [65536, 1536], P(('dp', 'sp')), parts along dimension 0
- output 2: bfloat16 [65536, 1536], P(('dp', 'sp')), parts along dimension 0
- output 3: float32 [6144, 1536], P('dp'), parts along dimension 0
- output 4: float32 [6144, 1536], P('dp'), parts along dimension 0
- output 5: float32 [6144, 1536], P('dp'), parts along dimension 0
- output 6: float32 [6144, 1536], P('dp'), parts along dimension 0
There are 4 independent parts. A program takes and returns all parts, laid end to end along the dimension named above; an argument that names none is the same for every part.
All inputs are finite; a program needn't handle non-finite values.
Results may differ from a plain program's by a relative error of at most 0.00435663.
Values are sent between devices in bfloat16 or wider.
A program may use at most 768 MiB of HBM per device.

v0:
```python
import math
import jax
import jax.numpy as jnp
from jax import lax
from jax.sharding import PartitionSpec as P

HEAD_DIM = 128
BLOCK_LEN = 128


def solution(mesh):
    n_seq = mesh.shape["sp"]
    fwd_perm = [(j, j + 1) for j in range(n_seq - 1)]
    rev_perm = [(j + 1, j) for j in range(n_seq - 1)]
    row_spec = P(("dp", "sp"), None)
    grad_spec = P("dp", None)

    def local_layer(tokens, w_q, w_k, w_v, w_o, grad_y):
        n_rows, model_dim = tokens.shape
        n_heads = model_dim // HEAD_DIM
        n_blocks = n_rows // BLOCK_LEN
        att_scale = 1.0 / math.sqrt(n_rows * n_seq * HEAD_DIM)
        causal = jnp.arange(BLOCK_LEN)[:, None] >= jnp.arange(BLOCK_LEN)[None, :]

        def project(operand, weight):
            return jnp.dot(operand, weight, preferred_element_type=jnp.float32).astype(jnp.bfloat16)

        def back_proj(rows, weight):
            return jnp.einsum("ne,de->nd", rows, weight, preferred_element_type=jnp.float32)

        def weight_grad(left_rows, right_rows):
            return jnp.einsum("nd,ne->de", left_rows, right_rows, preferred_element_type=jnp.float32)

        def split_heads(tensor):
            return tensor.reshape(n_blocks, BLOCK_LEN, n_heads, HEAD_DIM)

        def to_rows(tensor):
            return (tensor * att_scale).astype(jnp.bfloat16).reshape(n_rows, model_dim)

        q_heads = split_heads(project(tokens, w_q))
        k_heads = split_heads(project(tokens, w_k))
        v_heads = split_heads(project(tokens, w_v))
        block_kv = jnp.einsum("nshd,nshe->nhde", k_heads, v_heads, preferred_element_type=jnp.float32)
        kv_total = jnp.sum(block_kv, axis=0)

        def fwd_hop(hop_index, carried):
            return lax.ppermute(carried + kv_total, "sp", perm=fwd_perm)

        kv_in = lax.fori_loop(0, n_seq - 1, fwd_hop, jnp.zeros_like(kv_total))
        fwd_state = (kv_in + jnp.cumsum(block_kv, axis=0) - block_kv).astype(jnp.bfloat16)
        scores = jnp.einsum("nthd,nshd->nhts", q_heads, k_heads, preferred_element_type=jnp.float32)
        masked_scores = jnp.where(causal, scores, 0.0).astype(jnp.bfloat16)
        out_rows = to_rows(jnp.einsum("nhts,nshe->nthe", masked_scores, v_heads, preferred_element_type=jnp.float32) + jnp.einsum("nthd,nhde->nthe", q_heads, fwd_state, preferred_element_type=jnp.float32))
        out_y = project(out_rows, w_o)

        do_heads = split_heads(back_proj(grad_y, w_o).astype(jnp.bfloat16))
        block_qdo = jnp.einsum("nthd,nthe->nhde", q_heads, do_heads, preferred_element_type=jnp.float32)
        qdo_total = jnp.sum(block_qdo, axis=0)

        def rev_hop(hop_index, carried):
            return lax.ppermute(carried + qdo_total, "sp", perm=rev_perm)

        qdo_in = lax.fori_loop(0, n_seq - 1, rev_hop, jnp.zeros_like(qdo_total))
        rev_state = (qdo_in + qdo_total - jnp.cumsum(block_qdo, axis=0)).astype(jnp.bfloat16)
        d_scores = jnp.einsum("nthe,nshe->nhts", do_heads, v_heads, preferred_element_type=jnp.float32)
        masked_grads = jnp.where(causal, d_scores, 0.0).astype(jnp.bfloat16)
        dq_rows = to_rows(jnp.einsum("nhts,nshd->nthd", masked_grads, k_heads, preferred_element_type=jnp.float32) + jnp.einsum("nthe,nhde->nthd", do_heads, fwd_state, preferred_element_type=jnp.float32))
        dk_rows = to_rows(jnp.einsum("nhts,nthd->nshd", masked_grads, q_heads, preferred_element_type=jnp.float32) + jnp.einsum("nshe,nhde->nshd", v_heads, rev_state, preferred_element_type=jnp.float32))
        dv_rows = to_rows(jnp.einsum("nhts,nthe->nshe", masked_scores, do_heads, preferred_element_type=jnp.float32) + jnp.einsum("nshd,nhde->nshe", k_heads, rev_state, preferred_element_type=jnp.float32))
        grad_x = (back_proj(dq_rows, w_q) + back_proj(dk_rows, w_k) + back_proj(dv_rows, w_v)).astype(jnp.bfloat16)
        grads = lax.psum((weight_grad(tokens, dq_rows), weight_grad(tokens, dk_rows), weight_grad(tokens, dv_rows), weight_grad(out_rows, grad_y)), "sp")
        return (out_y, grad_x) + tuple(grads)

    return jax.shard_map(local_layer, mesh=mesh, in_specs=(row_spec, P(), P(), P(), P(), row_spec), out_specs=(row_spec, row_spec, grad_spec, grad_spec, grad_spec, grad_spec), check_vma=False)
```

profile of v0, /device:TPU:21, one launch (start us, length us, event | category | flops | bytes accessed | tf_op | source)
XLA Modules:
  0.0 1167.0 jit_solution(9094111279387841095)
XLA Ops:
  69.3 9.2 convolution_convert_fusion
  129.7 236.0 %while.20 = (s32[]{:T(128)}, f32[12,128,128]{2,1,0:T(8,128)}, f32[12,128,128]{2,1,0:T(8,128)}, s32[]{:T(128)}) while((s32[]{:T(128)}, f32[12,128,128]{2,1,0:T(8,128)}, f32[12,128,128]{2,1,0:T(8,128)}, s32[]{:T(128)}) %tuple.39), condition=%wide.region_2.0_spmd, body=%wide.region_1.0_spmd.sunk | while | flops 196610 | bytes 5505117 | solution.py:49
  153.2 8.9 collective-permute-done
  168.9 8.9 collective-permute-done
  200.2 8.9 collective-permute-done
  215.9 8.9 collective-permute-done
  231.5 8.9 collective-permute-done
  247.2 8.9 collective-permute-done
  278.5 8.9 collective-permute-done
  398.4 237.3 %while.21 = (s32[]{:T(128)}, f32[12,128,128]{2,1,0:T(8,128)}, f32[12,128,128]{2,1,0:T(8,128)}, s32[]{:T(128)}) while((s32[]{:T(128)}, f32[12,128,128]{2,1,0:T(8,128)}, f32[12,128,128]{2,1,0:T(8,128)}, s32[]{:T(128)}) %tuple.42), condition=%wide.region_6.7_spmd, body=%wide.region_5.6_spmd.sunk | while | flops 196610 | bytes 5505117 | solution.py:63
  402.7 12.1 %collective-permute-done.1 = f32[12,128,128]{2,1,0:T(8,128)} collective-permute-done((f32[12,128,128]{2,1,0:T(8,128)}, f32[12,128,128]{2,1,0:T(8,128)}, u32[]{:S(2)}, u32[]{:S(2)}) %collective-permute-start.1) | collective-permute-done | bytes 786464 | tf_op jit(solution)/shard_map/while/body/eval_jaxpr/ppermute | solution.py:61
  419.1 11.4 collective-permute-done.1
  434.8 11.4 collective-permute-done.1
  450.4 11.4 collective-permute-done.1
  466.1 11.4 collective-permute-done.1
  481.8 11.4 collective-permute-done.1
  497.4 11.4 collective-permute-done.1
  513.1 11.4 collective-permute-done.1
  528.8 11.4 collective-permute-done.1
  544.4 11.4 collective-permute-done.1
  560.1 11.4 collective-permute-done.1
  575.7 11.4 collective-permute-done.1
  591.4 11.4 collective-permute-done.1
  607.1 11.7 %collective-permute-done.1 = f32[12,128,128]{2,1,0:T(8,128)} collective-permute-done((f32[12,128,128]{2,1,0:T(8,128)}, f32[12,128,128]{2,1,0:T(8,128)}, u32[]{:S(2)}, u32[]{:S(2)}) %collective-permute-start.1) | collective-permute-done | bytes 786464 | tf_op jit(solution)/shard_map/while/body/eval_jaxpr/ppermute | solution.py:61
  623.0 12.6 %collective-permute-done.1 = f32[12,128,128]{2,1,0:T(8,128)} collective-permute-done((f32[12,128,128]{2,1,0:T(8,128)}, f32[12,128,128]{2,1,0:T(8,128)}, u32[]{:S(2)}, u32[]{:S(2)}) %collective-permute-start.1) | collective-permute-done | bytes 786464 | tf_op jit(solution)/shard_map/while/body/eval_jaxpr/ppermute | solution.py:61
  692.3 9.0 convolution_convert_fusion.1
  701.3 9.5 fusion.7
  710.9 9.1 add_convert_fusion
  720.0 402.7 %all-reduce.3.cloned.1.call-done = (f32[1536,1536]{0,1:T(8,128)}, f32[1536,1536]{0,1:T(8,128)}, f32[1536,1536]{0,1:T(8,128)}, f32[1536,1536]{1,0:T(8,128)}) async-done(((f32[1536,1536]{0,1:T(8,128)}, f32[1536,1536]{0,1:T(8,128)}, f32[1536,1536]{0,1:T(8,128)}, f32[1536,1536]{1,0:T(8,128)}), (f32[1536,1536]{0,1:T(8,128)}, f32[1536,1536]{0,1:T(8,128)}, f32[1536,1536]{0,1:T(8,128)}, ...) | async-done | bytes 37748752 | tf_op jit(solution)/shard_map/psum | solution.py:71
  1122.7 9.6 copy.59
  1132.3 9.6 copy.60
  1141.9 9.6 copy.61
  (157 shorter events, 447.8 us)
Async XLA Ops:
  7.2 1115.5 %all-reduce.3.cloned.1.call-start = ((), (), s32[]{:S(2)}) async-start(), calls=%async_computation | async-start | bytes 75497472 | tf_op jit(solution)/shard_map/psum | solution.py:71
  132.5 14.0 %collective-permute-start = (f32[12,128,128]{2,1,0:T(8,128)}, f32[12,128,128]{2,1,0:T(8,128)}, u32[]{:S(2)}, u32[]{:S(2)}) collective-permute-start(f32[12,128,128]{2,1,0:T(8,128)} %add.83), channel_id=1, source_target_pairs={{0,1},{1,2},{2,3},{3,4},{4,5},{5,6},{6,7},{7,8},{8,9},{9,10},{10,1... | collective-permute-start | bytes 2359304 | tf_op jit(solution)/shard_map/while/body/eval_jaxpr/ppermute | solution.py:47
  148.8 13.3 %collective-permute-start = (f32[12,128,128]{2,1,0:T(8,128)}, f32[12,128,128]{2,1,0:T(8,128)}, u32[]{:S(2)}, u32[]{:S(2)}) collective-permute-start(f32[12,128,128]{2,1,0:T(8,128)} %add.83), channel_id=1, source_target_pairs={{0,1},{1,2},{2,3},{3,4},{4,5},{5,6},{6,7},{7,8},{8,9},{9,10},{10,1... | collective-permute-start | bytes 2359304 | tf_op jit(solution)/shard_map/while/body/eval_jaxpr/ppermute | solution.py:47
  164.4 13.3 %collective-permute-start = (f32[12,128,128]{2,1,0:T(8,128)}, f32[12,128,128]{2,1,0:T(8,128)}, u32[]{:S(2)}, u32[]{:S(2)}) collective-permute-start(f32[12,128,128]{2,1,0:T(8,128)} %add.83), channel_id=1, source_target_pairs={{0,1},{1,2},{2,3},{3,4},{4,5},{5,6},{6,7},{7,8},{8,9},{9,10},{10,1... | collective-permute-start | bytes 2359304 | tf_op jit(solution)/shard_map/while/body/eval_jaxpr/ppermute | solution.py:47
  180.1 13.3 %collective-permute-start = (f32[12,128,128]{2,1,0:T(8,128)}, f32[12,128,128]{2,1,0:T(8,128)}, u32[]{:S(2)}, u32[]{:S(2)}) collective-permute-start(f32[12,128,128]{2,1,0:T(8,128)} %add.83), channel_id=1, source_target_pairs={{0,1},{1,2},{2,3},{3,4},{4,5},{5,6},{6,7},{7,8},{8,9},{9,10},{10,1... | collective-permute-start | bytes 2359304 | tf_op jit(solution)/shard_map/while/body/eval_jaxpr/ppermute | solution.py:47
  195.8 13.3 %collective-permute-start = (f32[12,128,128]{2,1,0:T(8,128)}, f32[12,128,128]{2,1,0:T(8,128)}, u32[]{:S(2)}, u32[]{:S(2)}) collective-permute-start(f32[12,128,128]{2,1,0:T(8,128)} %add.83), channel_id=1, source_target_pairs={{0,1},{1,2},{2,3},{3,4},{4,5},{5,6},{6,7},{7,8},{8,9},{9,10},{10,1... | collective-permute-start | bytes 2359304 | tf_op jit(solution)/shard_map/while/body/eval_jaxpr/ppermute | solution.py:47
  211.4 13.3 %collective-permute-start = (f32[12,128,128]{2,1,0:T(8,128)}, f32[12,128,128]{2,1,0:T(8,128)}, u32[]{:S(2)}, u32[]{:S(2)}) collective-permute-start(f32[12,128,128]{2,1,0:T(8,128)} %add.83), channel_id=1, source_target_pairs={{0,1},{1,2},{2,3},{3,4},{4,5},{5,6},{6,7},{7,8},{8,9},{9,10},{10,1... | collective-permute-start | bytes 2359304 | tf_op jit(solution)/shard_map/while/body/eval_jaxpr/ppermute | solution.py:47
  227.1 13.3 %collective-permute-start = (f32[12,128,128]{2,1,0:T(8,128)}, f32[12,128,128]{2,1,0:T(8,128)}, u32[]{:S(2)}, u32[]{:S(2)}) collective-permute-start(f32[12,128,128]{2,1,0:T(8,128)} %add.83), channel_id=1, source_target_pairs={{0,1},{1,2},{2,3},{3,4},{4,5},{5,6},{6,7},{7,8},{8,9},{9,10},{10,1... | collective-permute-start | bytes 2359304 | tf_op jit(solution)/shard_map/while/body/eval_jaxpr/ppermute | solution.py:47
  242.7 13.3 %collective-permute-start = (f32[12,128,128]{2,1,0:T(8,128)}, f32[12,128,128]{2,1,0:T(8,128)}, u32[]{:S(2)}, u32[]{:S(2)}) collective-permute-start(f32[12,128,128]{2,1,0:T(8,128)} %add.83), channel_id=1, source_target_pairs={{0,1},{1,2},{2,3},{3,4},{4,5},{5,6},{6,7},{7,8},{8,9},{9,10},{10,1... | collective-permute-start | bytes 2359304 | tf_op jit(solution)/shard_map/while/body/eval_jaxpr/ppermute | solution.py:47
  258.4 13.3 %collective-permute-start = (f32[12,128,128]{2,1,0:T(8,128)}, f32[12,128,128]{2,1,0:T(8,128)}, u32[]{:S(2)}, u32[]{:S(2)}) collective-permute-start(f32[12,128,128]{2,1,0:T(8,128)} %add.83), channel_id=1, source_target_pairs={{0,1},{1,2},{2,3},{3,4},{4,5},{5,6},{6,7},{7,8},{8,9},{9,10},{10,1... | collective-permute-start | bytes 2359304 | tf_op jit(solution)/shard_map/while/body/eval_jaxpr/ppermute | solution.py:47
  274.1 13.3 %collective-permute-start = (f32[12,128,128]{2,1,0:T(8,128)}, f32[12,128,128]{2,1,0:T(8,128)}, u32[]{:S(2)}, u32[]{:S(2)}) collective-permute-start(f32[12,128,128]{2,1,0:T(8,128)} %add.83), channel_id=1, source_target_pairs={{0,1},{1,2},{2,3},{3,4},{4,5},{5,6},{6,7},{7,8},{8,9},{9,10},{10,1... | collective-permute-start | bytes 2359304 | tf_op jit(solution)/shard_map/while/body/eval_jaxpr/ppermute | solution.py:47
  289.7 13.3 %collective-permute-start = (f32[12,128,128]{2,1,0:T(8,128)}, f32[12,128,128]{2,1,0:T(8,128)}, u32[]{:S(2)}, u32[]{:S(2)}) collective-permute-start(f32[12,128,128]{2,1,0:T(8,128)} %add.83), channel_id=1, source_target_pairs={{0,1},{1,2},{2,3},{3,4},{4,5},{5,6},{6,7},{7,8},{8,9},{9,10},{10,1... | collective-permute-start | bytes 2359304 | tf_op jit(solution)/shard_map/while/body/eval_jaxpr/ppermute | solution.py:47
  305.4 13.3 %collective-permute-start = (f32[12,128,128]{2,1,0:T(8,128)}, f32[12,128,128]{2,1,0:T(8,128)}, u32[]{:S(2)}, u32[]{:S(2)}) collective-permute-start(f32[12,128,128]{2,1,0:T(8,128)} %add.83), channel_id=1, source_target_pairs={{0,1},{1,2},{2,3},{3,4},{4,5},{5,6},{6,7},{7,8},{8,9},{9,10},{10,1... | collective-permute-start | bytes 2359304 | tf_op jit(solution)/shard_map/while/body/eval_jaxpr/ppermute | solution.py:47
  321.0 13.3 %collective-permute-start = (f32[12,128,128]{2,1,0:T(8,128)}, f32[12,128,128]{2,1,0:T(8,128)}, u32[]{:S(2)}, u32[]{:S(2)}) collective-permute-start(f32[12,128,128]{2,1,0:T(8,128)} %add.83), channel_id=1, source_target_pairs={{0,1},{1,2},{2,3},{3,4},{4,5},{5,6},{6,7},{7,8},{8,9},{9,10},{10,1... | collective-permute-start | bytes 2359304 | tf_op jit(solution)/shard_map/while/body/eval_jaxpr/ppermute | solution.py:47
  336.7 13.3 %collective-permute-start = (f32[12,128,128]{2,1,0:T(8,128)}, f32[12,128,128]{2,1,0:T(8,128)}, u32[]{:S(2)}, u32[]{:S(2)}) collective-permute-start(f32[12,128,128]{2,1,0:T(8,128)} %add.83), channel_id=1, source_target_pairs={{0,1},{1,2},{2,3},{3,4},{4,5},{5,6},{6,7},{7,8},{8,9},{9,10},{10,1... | collective-permute-start | bytes 2359304 | tf_op jit(solution)/shard_map/while/body/eval_jaxpr/ppermute | solution.py:47
  352.4 13.3 %collective-permute-start = (f32[12,128,128]{2,1,0:T(8,128)}, f32[12,128,128]{2,1,0:T(8,128)}, u32[]{:S(2)}, u32[]{:S(2)}) collective-permute-start(f32[12,128,128]{2,1,0:T(8,128)} %add.83), channel_id=1, source_target_pairs={{0,1},{1,2},{2,3},{3,4},{4,5},{5,6},{6,7},{7,8},{8,9},{9,10},{10,1... | collective-permute-start | bytes 2359304 | tf_op jit(solution)/shard_map/while/body/eval_jaxpr/ppermute | solution.py:47
  400.7 14.1 %collective-permute-start.1 = (f32[12,128,128]{2,1,0:T(8,128)}, f32[12,128,128]{2,1,0:T(8,128)}, u32[]{:S(2)}, u32[]{:S(2)}) collective-permute-start(f32[12,128,128]{2,1,0:T(8,128)} %add.85), channel_id=1, source_target_pairs={{1,0},{2,1},{3,2},{4,3},{5,4},{6,5},{7,6},{8,7},{9,8},{10,9},{11,1... | collective-permute-start | bytes 2359304 | tf_op jit(solution)/shard_map/while/body/eval_jaxpr/ppermute | solution.py:61
  417.2 13.3 %collective-permute-start.1 = (f32[12,128,128]{2,1,0:T(8,128)}, f32[12,128,128]{2,1,0:T(8,128)}, u32[]{:S(2)}, u32[]{:S(2)}) collective-permute-start(f32[12,128,128]{2,1,0:T(8,128)} %add.85), channel_id=1, source_target_pairs={{1,0},{2,1},{3,2},{4,3},{5,4},{6,5},{7,6},{8,7},{9,8},{10,9},{11,1... | collective-permute-start | bytes 2359304 | tf_op jit(solution)/shard_map/while/body/eval_jaxpr/ppermute | solution.py:61
  432.8 13.3 %collective-permute-start.1 = (f32[12,128,128]{2,1,0:T(8,128)}, f32[12,128,128]{2,1,0:T(8,128)}, u32[]{:S(2)}, u32[]{:S(2)}) collective-permute-start(f32[12,128,128]{2,1,0:T(8,128)} %add.85), channel_id=1, source_target_pairs={{1,0},{2,1},{3,2},{4,3},{5,4},{6,5},{7,6},{8,7},{9,8},{10,9},{11,1... | collective-permute-start | bytes 2359304 | tf_op jit(solution)/shard_map/while/body/eval_jaxpr/ppermute | solution.py:61
  448.5 13.3 %collective-permute-start.1 = (f32[12,128,128]{2,1,0:T(8,128)}, f32[12,128,128]{2,1,0:T(8,128)}, u32[]{:S(2)}, u32[]{:S(2)}) collective-permute-start(f32[12,128,128]{2,1,0:T(8,128)} %add.85), channel_id=1, source_target_pairs={{1,0},{2,1},{3,2},{4,3},{5,4},{6,5},{7,6},{8,7},{9,8},{10,9},{11,1... | collective-permute-start | bytes 2359304 | tf_op jit(solution)/shard_map/while/body/eval_jaxpr/ppermute | solution.py:61
  464.2 13.3 %collective-permute-start.1 = (f32[12,128,128]{2,1,0:T(8,128)}, f32[12,128,128]{2,1,0:T(8,128)}, u32[]{:S(2)}, u32[]{:S(2)}) collective-permute-start(f32[12,128,128]{2,1,0:T(8,128)} %add.85), channel_id=1, source_target_pairs={{1,0},{2,1},{3,2},{4,3},{5,4},{6,5},{7,6},{8,7},{9,8},{10,9},{11,1... | collective-permute-start | bytes 2359304 | tf_op jit(solution)/shard_map/while/body/eval_jaxpr/ppermute | solution.py:61
  479.8 13.3 %collective-permute-start.1 = (f32[12,128,128]{2,1,0:T(8,128)}, f32[12,128,128]{2,1,0:T(8,128)}, u32[]{:S(2)}, u32[]{:S(2)}) collective-permute-start(f32[12,128,128]{2,1,0:T(8,128)} %add.85), channel_id=1, source_target_pairs={{1,0},{2,1},{3,2},{4,3},{5,4},{6,5},{7,6},{8,7},{9,8},{10,9},{11,1... | collective-permute-start | bytes 2359304 | tf_op jit(solution)/shard_map/while/body/eval_jaxpr/ppermute | solution.py:61
  495.5 13.3 %collective-permute-start.1 = (f32[12,128,128]{2,1,0:T(8,128)}, f32[12,128,128]{2,1,0:T(8,128)}, u32[]{:S(2)}, u32[]{:S(2)}) collective-permute-start(f32[12,128,128]{2,1,0:T(8,128)} %add.85), channel_id=1, source_target_pairs={{1,0},{2,1},{3,2},{4,3},{5,4},{6,5},{7,6},{8,7},{9,8},{10,9},{11,1... | collective-permute-start | bytes 2359304 | tf_op jit(solution)/shard_map/while/body/eval_jaxpr/ppermute | solution.py:61
  511.1 13.3 %collective-permute-start.1 = (f32[12,128,128]{2,1,0:T(8,128)}, f32[12,128,128]{2,1,0:T(8,128)}, u32[]{:S(2)}, u32[]{:S(2)}) collective-permute-start(f32[12,128,128]{2,1,0:T(8,128)} %add.85), channel_id=1, source_target_pairs={{1,0},{2,1},{3,2},{4,3},{5,4},{6,5},{7,6},{8,7},{9,8},{10,9},{11,1... | collective-permute-start | bytes 2359304 | tf_op jit(solution)/shard_map/while/body/eval_jaxpr/ppermute | solution.py:61
  526.8 13.3 %collective-permute-start.1 = (f32[12,128,128]{2,1,0:T(8,128)}, f32[12,128,128]{2,1,0:T(8,128)}, u32[]{:S(2)}, u32[]{:S(2)}) collective-permute-start(f32[12,128,128]{2,1,0:T(8,128)} %add.85), channel_id=1, source_target_pairs={{1,0},{2,1},{3,2},{4,3},{5,4},{6,5},{7,6},{8,7},{9,8},{10,9},{11,1... | collective-permute-start | bytes 2359304 | tf_op jit(solution)/shard_map/while/body/eval_jaxpr/ppermute | solution.py:61
  542.5 13.3 %collective-permute-start.1 = (f32[12,128,128]{2,1,0:T(8,128)}, f32[12,128,128]{2,1,0:T(8,128)}, u32[]{:S(2)}, u32[]{:S(2)}) collective-permute-start(f32[12,128,128]{2,1,0:T(8,128)} %add.85), channel_id=1, source_target_pairs={{1,0},{2,1},{3,2},{4,3},{5,4},{6,5},{7,6},{8,7},{9,8},{10,9},{11,1... | collective-permute-start | bytes 2359304 | tf_op jit(solution)/shard_map/while/body/eval_jaxpr/ppermute | solution.py:61
  558.1 13.3 %collective-permute-start.1 = (f32[12,128,128]{2,1,0:T(8,128)}, f32[12,128,128]{2,1,0:T(8,128)}, u32[]{:S(2)}, u32[]{:S(2)}) collective-permute-start(f32[12,128,128]{2,1,0:T(8,128)} %add.85), channel_id=1, source_target_pairs={{1,0},{2,1},{3,2},{4,3},{5,4},{6,5},{7,6},{8,7},{9,8},{10,9},{11,1... | collective-permute-start | bytes 2359304 | tf_op jit(solution)/shard_map/while/body/eval_jaxpr/ppermute | solution.py:61
  573.8 13.3 %collective-permute-start.1 = (f32[12,128,128]{2,1,0:T(8,128)}, f32[12,128,128]{2,1,0:T(8,128)}, u32[]{:S(2)}, u32[]{:S(2)}) collective-permute-start(f32[12,128,128]{2,1,0:T(8,128)} %add.85), channel_id=1, source_target_pairs={{1,0},{2,1},{3,2},{4,3},{5,4},{6,5},{7,6},{8,7},{9,8},{10,9},{11,1... | collective-permute-start | bytes 2359304 | tf_op jit(solution)/shard_map/while/body/eval_jaxpr/ppermute | solution.py:61
  589.4 13.3 %collective-permute-start.1 = (f32[12,128,128]{2,1,0:T(8,128)}, f32[12,128,128]{2,1,0:T(8,128)}, u32[]{:S(2)}, u32[]{:S(2)}) collective-permute-start(f32[12,128,128]{2,1,0:T(8,128)} %add.85), channel_id=1, source_target_pairs={{1,0},{2,1},{3,2},{4,3},{5,4},{6,5},{7,6},{8,7},{9,8},{10,9},{11,1... | collective-permute-start | bytes 2359304 | tf_op jit(solution)/shard_map/while/body/eval_jaxpr/ppermute | solution.py:61
  605.1 13.6 %collective-permute-start.1 = (f32[12,128,128]{2,1,0:T(8,128)}, f32[12,128,128]{2,1,0:T(8,128)}, u32[]{:S(2)}, u32[]{:S(2)}) collective-permute-start(f32[12,128,128]{2,1,0:T(8,128)} %add.85), channel_id=1, source_target_pairs={{1,0},{2,1},{3,2},{4,3},{5,4},{6,5},{7,6},{8,7},{9,8},{10,9},{11,1... | collective-permute-start | bytes 2359304 | tf_op jit(solution)/shard_map/while/body/eval_jaxpr/ppermute | solution.py:61
  621.1 14.5 %collective-permute-start.1 = (f32[12,128,128]{2,1,0:T(8,128)}, f32[12,128,128]{2,1,0:T(8,128)}, u32[]{:S(2)}, u32[]{:S(2)}) collective-permute-start(f32[12,128,128]{2,1,0:T(8,128)} %add.85), channel_id=1, source_target_pairs={{1,0},{2,1},{3,2},{4,3},{5,4},{6,5},{7,6},{8,7},{9,8},{10,9},{11,1... | collective-permute-start | bytes 2359304 | tf_op jit(solution)/shard_map/while/body/eval_jaxpr/ppermute | solution.py:61
  692.3 18.6 %slice-start.2 = ((s8[4718592]{0:T(1024)(128)(4,1)}), s8[4194304]{0:T(1024)(128)(4,1)S(1)}, s32[]{:S(2)}) async-start(s8[4718592]{0:T(1024)(128)(4,1)} %bitcast.105), calls=%async_computation.3 | async-start | bytes 8388608
  (22 other events, 157.6 us)
Sparse Core Ops, SparseCore 0:
  684.2 438.4 all-reduce.2
where the time goes:
time: 1180 us; the launch traced here: 1170 us
  waiting for transfers between devices  709 us (60%)
  matrix products  156 us (13%)
  local copies, waits for them, and re-layouts  104 us (9%)
  starting transfers between devices  96.3 us (8%)
  other arithmetic  85.5 us (7%)
  between operations  14.8 us (1%)
    psum x1, waiting for transfers between devices, local_layer(): lax.psum((weight_grad(tokens, dq_rows), weight_grad(tokens, dk_rows), wei...  403 us
    ppermute x15, waiting for transfers between devices, rev_hop(): return lax.ppermute(carried + qdo_total, 'sp', perm=rev_perm)  173 us
    ppermute x15, waiting for transfers between devices, fwd_hop(): return lax.ppermute(carried + kv_total, 'sp', perm=fwd_perm)  133 us
    ppermute x15, starting transfers between devices, fwd_hop(): return lax.ppermute(carried + kv_total, 'sp', perm=fwd_perm)  67.1 us
    unnamed x51, local copies, waits for them, and re-layouts  47.2 us
    reshape x6, local copies, waits for them, and re-layouts, split_heads(): return tensor.reshape(n_blocks, BLOCK_LEN, n_heads, HEAD_DIM)  38.7 us
    dot_general x4, matrix products, back_proj(): jnp.einsum('ne,de->nd', rows, weight, preferred_element_type=jnp.float32)  36.1 us
    dot_general x4, matrix products, project(): jnp.dot(operand, weight, preferred_element_type=jnp.float32)  35.1 us
  transfers between devices with their start and end apart: 31, of which 31 were waited for; matrix products, arithmetic and copies ran while one was open for 3% of the time, Pallas kernels for 0%

commit v1 on v0

v1 whole, which is shorter than its diff:
```python
import functools
import math
import jax
import jax.numpy as jnp
from jax import lax
from jax.experimental import pallas as pl
from jax.experimental.pallas import tpu as pltpu
from jax.sharding import PartitionSpec as P

HEAD_DIM = 128
BLOCK_LEN = 128
TILE = 128
ROWS = 256
MESH = pl.DeviceIdType.MESH
VMEM_LIMIT = 67_043_328
F32 = jnp.float32
BF16 = jnp.bfloat16


def dot_t(lhs, rhs):
    return lax.dot_general(lhs, rhs, (((0,), (0,)), ((), ())), preferred_element_type=F32)


def dot_nt(lhs, rhs):
    return lax.dot_general(lhs, rhs, (((1,), (1,)), ((), ())), preferred_element_type=F32)


def dot(lhs, rhs):
    return jnp.dot(lhs, rhs, preferred_element_type=F32)


def aligned(index, size):
    return pl.ds(pl.multiple_of(index * size, size), size)


def position(n_seq):
    me = lax.axis_index("sp")
    core, chip = lax.rem(me, 2), lax.div(me, 2)
    return core, chip, n_seq // 2, me + 1 - 2 * core


def send(src, dst, send_sem, recv_sem, target):
    return pltpu.make_async_remote_copy(src_ref=src, dst_ref=dst, send_sem=send_sem, recv_sem=recv_sem, device_id={"sp": target}, device_id_type=MESH)


def entry_barrier(targets):
    barrier = pltpu.get_barrier_semaphore()
    for target in targets:
        pl.semaphore_signal(barrier, inc=1, device_id={"sp": target}, device_id_type=MESH)
    pl.semaphore_wait(barrier, len(targets))


def attention_kernel(n_seq, scale, x, dy, wq, wk, wv, wo, xo_out, ra_out, xf, dyf, w_s, wo_s, q, k, v, do, o, dq, a_s, b_s, kv_s, qdo_s, s_in, s_out, r_in, r_out, x_sems, w_sems, chain_sems, out_sems):
    core, chip, n_chips, peer = position(n_seq)
    me = lax.axis_index("sp")
    up, down = lax.rem(me + 2, n_seq), lax.rem(me + n_seq - 2, n_seq)
    n_rows, dim = x.shape
    all_rows, width = q.shape
    n_heads = width // HEAD_DIM
    n_blocks = all_rows // BLOCK_LEN
    own_rows = aligned(core, n_rows)

    entry_barrier((peer, up, down))
    local = []
    remote = []
    for index, (src, dst) in enumerate(((x, xf), (dy, dyf))):
        remote.append(send(src, dst.at[own_rows], x_sems.at[index, 0], x_sems.at[index, 1], peer))
        local.append(pltpu.make_async_copy(src, dst.at[own_rows], x_sems.at[index, 2]))
    w_cols = aligned(core, width)
    w_loads = [pltpu.make_async_copy(weight.at[:, w_cols], w_s.at[index], w_sems.at[index]) for index, weight in enumerate((wk, wv, wq))]
    w_loads.append(pltpu.make_async_copy(wo.at[w_cols], wo_s, w_sems.at[3]))
    remote[0].start()
    local[0].start()
    for load in w_loads[:2]:
        load.start()
    remote[1].start()
    for load in w_loads[2:]:
        load.start()
    local[1].start()

    def project(half, jobs):
        @pl.loop(0, n_rows // ROWS)
        def _(step):
            rows = pl.ds(pl.multiple_of(half * n_rows + step * ROWS, ROWS), ROWS)
            for src, weight, dst, transposed in jobs:
                product = dot_nt(src[rows, :], weight[...]) if transposed else dot(src[rows, :], weight[...])
                dst[rows, :] = product.astype(BF16)

    kv_jobs = ((xf, w_s.at[0], k, False), (xf, w_s.at[1], v, False))
    qo_jobs = ((xf, w_s.at[2], q, False), (dyf, wo_s, do, True))
    local[0].wait()
    w_loads[0].wait()
    w_loads[1].wait()
    project(core, kv_jobs)
    remote[0].wait()
    project(1 - core, kv_jobs)

    def accumulate(lhs, rhs, kept, total, reverse):
        total[...] = jnp.zeros_like(total)

        @pl.loop(0, n_blocks)
        def _(step):
            block = (n_blocks - 1 - step) if reverse else step
            rows = aligned(block, BLOCK_LEN)
            for h in range(n_heads):
                cols = pl.ds(h * HEAD_DIM, HEAD_DIM)
                running = total[h]
                kept[block, h] = running
                total[h] = running + dot_t(lhs[rows, cols], rhs[rows, cols])

    accumulate(k, v, kv_s, s_out, False)
    local[1].wait()
    w_loads[2].wait()
    w_loads[3].wait()
    project(core, qo_jobs)
    remote[1].wait()
    project(1 - core, qo_jobs)
    accumulate(q, do, qdo_s, r_out, True)

    x_out = pltpu.make_async_copy(xf, xo_out.at[:, pl.ds(0, dim)], out_sems.at[0])
    dy_out = pltpu.make_async_copy(dyf, ra_out.at[:, pl.ds(width, dim)], out_sems.at[1])
    x_out.start()
    dy_out.start()

    def chain_copy(which, h):
        src, dst, target = ((s_out, s_in, up), (r_out, r_in, down))[which]
        return send(src.at[h], dst.at[h], chain_sems.at[which, 0, h], chain_sems.at[which, 1, h], target)

    def chain_step(which, h):
        first, last = ((0, n_chips - 1), (n_chips - 1, 0))[which]
        src, dst = ((s_out, s_in), (r_out, r_in))[which]

        @pl.when(chip == first)
        def _():
            dst[h] = jnp.zeros_like(dst[h])

        @pl.when(chip != first)
        def _():
            chain_copy(which, h).wait_recv()
            src[h] = src[h] + dst[h]

        @pl.when(chip != last)
        def _():
            chain_copy(which, h).start()

    high = lax.div(chip, n_chips // 2)
    lag_s = high * 2 * (2 * chip - (n_chips - 1))
    lag_r = (1 - high) * 2 * ((n_chips - 1) - 2 * chip)

    causal = lax.broadcasted_iota(jnp.int32, (BLOCK_LEN, BLOCK_LEN), 0) >= lax.broadcasted_iota(jnp.int32, (BLOCK_LEN, BLOCK_LEN), 1)

    def block_scores(block):
        rows = aligned(block, BLOCK_LEN)
        for h in range(n_heads):
            cols = pl.ds(h * HEAD_DIM, HEAD_DIM)
            a_s[block, h] = jnp.where(causal, dot_nt(q[rows, cols], k[rows, cols]), 0.0).astype(BF16)
            b_s[block, h] = jnp.where(causal, dot_nt(do[rows, cols], v[rows, cols]), 0.0).astype(BF16)

    @pl.loop(0, max(n_heads + 2 * (n_chips - 1), n_blocks))
    def _(step):
        for which, lag in ((0, lag_s), (1, lag_r)):
            @pl.when((step >= lag) & (step < lag + n_heads))
            def _():
                chain_step(which, step - lag)

        @pl.when(step < n_blocks)
        def _():
            block_scores(step)

    @pl.loop(0, n_blocks)
    def _(block):
        rows = aligned(block, BLOCK_LEN)
        for h in range(n_heads):
            cols = pl.ds(h * HEAD_DIM, HEAD_DIM)
            qb, kb, vb, dob = q[rows, cols], k[rows, cols], v[rows, cols], do[rows, cols]
            a, b = a_s[block, h], b_s[block, h]
            s = (s_in[h] + kv_s[block, h]).astype(BF16)
            r = (r_in[h] + qdo_s[block, h]).astype(BF16)

            def both(left, right, top, bottom):
                out = dot(jnp.concatenate([left, right], axis=1), jnp.concatenate([top, bottom], axis=0))
                return (out * scale).astype(BF16)

            o[rows, cols] = both(a, qb, vb, s)
            dq[rows, cols] = both(b, dob, kb, s.T)
            k[rows, cols] = both(b.T, vb, qb, r.T)
            v[rows, cols] = both(a.T, kb, dob, r)

    outs = [pltpu.make_async_copy(o, xo_out.at[:, pl.ds(dim, width)], out_sems.at[2])]
    for index, (src, column) in enumerate(((dq, 0), (k, width + dim), (v, 2 * width + dim))):
        outs.append(pltpu.make_async_copy(src, ra_out.at[:, pl.ds(column, width)], out_sems.at[3 + index]))
    for copy in outs:
        copy.start()
    for which, last in ((0, n_chips - 1), (1, 0)):
        @pl.when(chip != last)
        def _():
            for h in range(n_heads):
                chain_copy(which, h).wait_send()
    for copy in outs + [x_out, dy_out]:
        copy.wait()


def ring(n_seq):
    core, chip, n_chips, peer = position(n_seq)
    me = lax.axis_index("sp")
    rank = (1 - core) * chip + core * lax.rem(n_chips - chip, n_chips)
    following = lax.rem(me + 2 - 4 * core + n_seq, n_seq)
    previous = lax.rem(me - 2 + 4 * core + n_seq, n_seq)
    return core, rank, n_chips, peer, following, previous


def tile_slot(chunk, piece, early):
    return chunk * early + lax.rem(piece, early), lax.div(piece, early)


def reduce_kernel(n_seq, xo, ra, red_out, own_out, grads, red, send_sems, recv_sems, own_sems, out_sem):
    core, rank, n_chips, peer, following, previous = ring(n_seq)
    n_slots, _, width = grads.shape
    dim = 2 * width
    per_weight = dim // TILE
    early = 2 * per_weight // n_chips
    pieces = 2 * early
    n_rows = own_out.shape[1]

    entry_barrier((peer, following, previous))
    own_rows, peer_rows = aligned(core, n_rows), aligned(1 - core, n_rows)
    cols = aligned(core, width)
    copies = []
    for index, (src, column) in enumerate(((xo, dim), (ra, 0), (ra, width + dim), (ra, 2 * width + dim))):
        part = pl.ds(column, width)
        copies.append(pltpu.make_async_copy(src.at[own_rows, part], own_out.at[index, :, cols], own_sems.at[index, 0]))
        copies.append(send(src.at[peer_rows, part], own_out.at[index, :, cols], own_sems.at[index, 1], own_sems.at[index, 2], peer))

    def term(chunk, piece):
        unit, late = tile_slot(chunk, piece, early)
        inside = lax.rem(unit, per_weight)
        second = lax.div(unit, per_weight)
        is_o = (1 - late) * second
        left = (1 - is_o) * inside + is_o * (per_weight + lax.div(inside, 2))
        right = (1 - late) * is_o * (1 + lax.rem(inside, 2)) + late * (3 + second)
        return dot_t(xo[:, aligned(left, TILE)], ra[:, aligned(right, width)])

    def slot_of(chunk, piece):
        unit, late = tile_slot(chunk, piece, early)
        return unit + late * (n_slots // 2)

    def hop(step, piece):
        slot = slot_of(lax.rem(rank - step + n_chips, n_chips), piece)
        return send(grads.at[slot], grads.at[slot], send_sems.at[step, piece], recv_sems.at[step, piece], following)

    def arrival(step, piece):
        slot = slot_of(lax.rem(rank - step - 1 + n_chips, n_chips), piece)
        return send(grads.at[slot], grads.at[slot], send_sems.at[step, piece], recv_sems.at[step, piece], following)

    @pl.loop(0, pieces)
    def _(piece):
        grads[slot_of(rank, piece)] = term(rank, piece)
        hop(0, piece).start()

    for copy in copies:
        copy.start()

    @pl.loop(1, n_chips)
    def _(step):
        @pl.loop(0, pieces)
        def _(piece):
            chunk = lax.rem(rank - step + n_chips, n_chips)
            slot = slot_of(chunk, piece)
            mine = term(chunk, piece)
            arrival(step - 1, piece).wait_recv()

            @pl.when(step < n_chips - 1)
            def _():
                grads[slot] = grads[slot] + mine
                hop(step, piece).start()

            @pl.when(step == n_chips - 1)
            def _():
                red[piece] = grads[slot] + mine

    result = pltpu.make_async_copy(red, red_out, out_sem)
    result.start()

    @pl.loop(0, n_chips - 1)
    def _(step):
        @pl.loop(0, pieces)
        def _(piece):
            hop(step, piece).wait_send()

    for copy in copies:
        copy.wait()
    result.wait()


def gather_kernel(n_seq, red, own, wq, wk, wv, wo, both_out, y_out, dx_out, own_s, wo_s, w_s, y_s, dx_s, own_sems, w_sems, res_sems, send_sems, recv_sems, peer_sems):
    core, rank, n_chips, peer, following, previous = ring(n_seq)
    mine_out, peer_out = both_out.at[0], both_out.at[1]
    n_slots, _, width = mine_out.shape
    dim = 2 * width
    early = 2 * (dim // TILE) // n_chips
    pieces = 2 * early
    n_rows = own.shape[1]
    unit_cols = wo_s.shape[2]
    n_units = dim // unit_cols
    row_blocks = n_rows // ROWS

    def slot_of(chunk, piece):
        unit, late = tile_slot(chunk, piece, early)
        return unit + late * (n_slots // 2)

    def held(step, piece):
        return slot_of(lax.rem(rank + 1 - step + n_chips, n_chips), piece)

    def w_loads(unit, buffer):
        part = aligned(unit, unit_cols)
        loads = [pltpu.make_async_copy(wo.at[:, part], wo_s.at[buffer], w_sems.at[buffer, 0])]
        for index, weight in enumerate((wq, wk, wv)):
            loads.append(pltpu.make_async_copy(weight.at[part], w_s.at[buffer, index], w_sems.at[buffer, 1 + index]))
        return loads

    def results(unit, buffer):
        part = aligned(unit, unit_cols)
        return [pltpu.make_async_copy(src.at[buffer], dst.at[:, part], res_sems.at[buffer, index]) for index, (src, dst) in enumerate(((y_s, y_out), (dx_s, dx_out)))]

    own_load = pltpu.make_async_copy(own, own_s, own_sems.at[0])
    own_load.start()
    for unit in range(2):
        for load in w_loads(unit, unit):
            load.start()
    red_loads = [pltpu.make_async_copy(red.at[piece], mine_out.at[held(0, piece)], own_sems.at[1 + piece]) for piece in range(pieces)]
    for load in red_loads:
        load.start()

    entry_barrier((peer, following, previous))

    def to_next(step, piece):
        slot = held(step, piece)
        return send(mine_out.at[slot], mine_out.at[slot], send_sems.at[step, piece], recv_sems.at[step, piece], following)

    def arrival(step, piece):
        slot = held(step + 1, piece)
        return send(mine_out.at[slot], mine_out.at[slot], send_sems.at[step, piece], recv_sems.at[step, piece], following)

    def to_peer(step, piece):
        slot = held(step, piece)
        return send(mine_out.at[slot], peer_out.at[slot], peer_sems.at[0, step, piece], peer_sems.at[1, step, piece], peer)

    for piece in range(pieces):
        red_loads[piece].wait()
        to_next(0, piece).start()
        to_peer(0, piece).start()
    own_load.wait()

    def project(unit, block):
        buffer = lax.rem(unit, 2)

        @pl.when(block == 0)
        def _():
            for load in w_loads(unit, buffer):
                load.wait()

            @pl.when(unit >= 2)
            def _():
                for copy in results(unit - 2, buffer):
                    copy.wait()

        rows = aligned(block, ROWS)
        y_s[buffer, rows, :] = dot(own_s[0, rows, :], wo_s[buffer]).astype(BF16)
        total = dot_nt(own_s[1, rows, :], w_s[buffer, 0])
        total += dot_nt(own_s[2, rows, :], w_s[buffer, 1])
        total += dot_nt(own_s[3, rows, :], w_s[buffer, 2])
        dx_s[buffer, rows, :] = total.astype(BF16)

        @pl.when(block == row_blocks - 1)
        def _():
            for copy in results(unit, buffer):
                copy.start()

            @pl.when(unit + 2 < n_units)
            def _():
                for load in w_loads(unit + 2, buffer):
                    load.start()

    @pl.loop(0, (n_chips - 1) * pieces)
    def _(index):
        step, piece = lax.div(index, pieces), lax.rem(index, pieces)

        @pl.when(index < n_units * row_blocks)
        def _():
            project(lax.div(index, row_blocks), lax.rem(index, row_blocks))

        arrival(step, piece).wait_recv()

        @pl.when(step < n_chips - 2)
        def _():
            to_next(step + 1, piece).start()

        to_peer(step + 1, piece).start()

    @pl.loop(0, n_chips * pieces)
    def _(index):
        step, piece = lax.div(index, pieces), lax.rem(index, pieces)

        @pl.when(step < n_chips - 1)
        def _():
            to_next(step, piece).wait_send()

        to_peer(step, piece).wait()

    for unit in range(n_units - 2, n_units):
        for copy in results(unit, unit % 2):
            copy.wait()


def place_kernel(both, gq, gk, gv, go, sems):
    core = lax.rem(lax.axis_index("sp"), 2)
    _, n_slots, _, width = both.shape
    per_weight = n_slots // 4
    copies = []
    for side, half in enumerate((core, 1 - core)):
        cols = aligned(half, width)
        for slot in range(n_slots):
            weight, inside = slot // per_weight, slot % per_weight
            if weight == 1:
                rows = pl.ds(pl.multiple_of(half * width + inside // 2 * TILE, TILE), TILE)
                dst = go.at[rows, pl.ds(inside % 2 * width, width)]
            else:
                dst = (gq, None, gk, gv)[weight].at[pl.ds(inside * TILE, TILE), cols]
            copies.append(pltpu.make_async_copy(both.at[side, slot], dst, sems.at[side]))
    for copy in copies:
        copy.start()
    for copy in copies:
        copy.wait()


def solution(mesh):
    n_seq = mesh.shape["sp"]
    n_chips = n_seq // 2
    row_spec = P(("dp", "sp"), None)
    grad_spec = P("dp", None)
    any_spec = pl.BlockSpec(memory_space=pl.ANY)
    vmem_spec = pl.BlockSpec(memory_space=pltpu.VMEM)
    dma = pltpu.SemaphoreType.DMA

    def params(collective_id, limit=VMEM_LIMIT):
        return pltpu.CompilerParams(collective_id=collective_id, has_side_effects=True, vmem_limit_bytes=limit)

    def local_layer(tokens, w_q, w_k, w_v, w_o, grad_y):
        n_rows, dim = tokens.shape
        width = dim // 2
        n_heads = width // HEAD_DIM
        rows = 2 * n_rows
        n_blocks = rows // BLOCK_LEN
        n_slots = 4 * (dim // TILE)
        pieces = n_slots // n_chips
        scale = 1.0 / math.sqrt(n_rows * n_seq * HEAD_DIM)
        state = (n_heads, HEAD_DIM, HEAD_DIM)

        xo, ra = pl.pallas_call(
            functools.partial(attention_kernel, n_seq, scale),
            out_shape=(jax.ShapeDtypeStruct((rows, dim + width), BF16), jax.ShapeDtypeStruct((rows, dim + 3 * width), BF16)),
            in_specs=[any_spec] * 6,
            out_specs=(any_spec,) * 2,
            scratch_shapes=[pltpu.VMEM((rows, dim), BF16)] * 2
            + [pltpu.VMEM((3, dim, width), BF16), pltpu.VMEM((width, dim), BF16)]
            + [pltpu.VMEM((rows, width), BF16)] * 6
            + [pltpu.VMEM((n_blocks, n_heads, BLOCK_LEN, BLOCK_LEN), BF16)] * 2
            + [pltpu.VMEM((n_blocks,) + state, F32)] * 2
            + [pltpu.VMEM(state, F32)] * 4
            + [dma((2, 3)), dma((4,)), dma((2, 2, n_heads)), dma((6,))],
            compiler_params=params(0),
            name="attention",
        )(tokens, grad_y, w_q, w_k, w_v, w_o)

        red, own = pl.pallas_call(
            functools.partial(reduce_kernel, n_seq),
            out_shape=(jax.ShapeDtypeStruct((pieces, TILE, width), F32), jax.ShapeDtypeStruct((4, n_rows, dim), BF16)),
            in_specs=[vmem_spec] * 2,
            out_specs=(any_spec,) * 2,
            scratch_shapes=[pltpu.VMEM((n_slots, TILE, width), F32), pltpu.VMEM((pieces, TILE, width), F32)]
            + [dma((n_chips - 1, pieces))] * 2 + [dma((4, 3)), dma],
            compiler_params=params(1),
            name="reduce",
        )(xo, ra)

        unit_cols = min(256, dim // 2)
        halves = (2, n_slots, TILE, width)
        both, out_y, grad_x = pl.pallas_call(
            functools.partial(gather_kernel, n_seq),
            out_shape=(pltpu.VMEM(halves, F32), jax.ShapeDtypeStruct((n_rows, dim), BF16), jax.ShapeDtypeStruct((n_rows, dim), BF16)),
            in_specs=[any_spec] * 6,
            out_specs=(vmem_spec, any_spec, any_spec),
            scratch_shapes=[pltpu.VMEM((4, n_rows, dim), BF16), pltpu.VMEM((2, dim, unit_cols), BF16), pltpu.VMEM((2, 3, unit_cols, dim), BF16)]
            + [pltpu.VMEM((2, n_rows, unit_cols), BF16)] * 2
            + [dma((1 + pieces,)), dma((2, 4)), dma((2, 2)), dma((n_chips - 1, pieces)), dma((n_chips - 1, pieces)), dma((2, n_chips, pieces))],
            compiler_params=params(2, VMEM_LIMIT - math.prod(halves) * 4 - (1 << 20)),
            name="gather",
        )(red, own, w_q, w_k, w_v, w_o)

        grads = pl.pallas_call(
            place_kernel,
            out_shape=(jax.ShapeDtypeStruct((dim, dim), F32),) * 4,
            in_specs=[vmem_spec],
            out_specs=(any_spec,) * 4,
            scratch_shapes=[dma((2,))],
            compiler_params=pltpu.CompilerParams(vmem_limit_bytes=1 << 20),
            name="place",
        )(both)
        return (out_y, grad_x) + tuple(grads)

    return jax.shard_map(local_layer, mesh=mesh, in_specs=(row_spec, P(), P(), P(), P(), row_spec), out_specs=(row_spec, row_spec, grad_spec, grad_spec, grad_spec, grad_spec), check_vma=False)
```

time: 1180 us -> 490 us (0.42); the launches traced: 1170 us -> 489 us
  waiting for transfers between devices: 709 us -> 0 us
  Pallas kernels: 0 us -> 483 us
  matrix products: 156 us -> 0 us
  local copies, waits for them, and re-layouts: 104 us -> 5.59 us
  starting transfers between devices: 96.3 us -> 0 us
  other arithmetic: 85.5 us -> 0 us
  between operations: 14.8 us -> 0.67 us
    pallas_call x0 -> x4, Pallas kernels: none -> 483 us  [the longest x1 194 us: local_layer(): pl.pallas_call(functools.partial(gather_kernel, n_seq), out_shape=(pltpu....]
    psum x1 -> x0, waiting for transfers between devices: 403 us -> none  [local_layer(): lax.psum((weight_grad(tokens, dq_rows), weight_grad(tokens, dk_rows), wei...]
    ppermute x30 -> x0, waiting for transfers between devices: 306 us -> none  [the longest x15 173 us: rev_hop(): return lax.ppermute(carried + qdo_total, 'sp', perm=rev_perm)]
    dot_general x24 -> x0, matrix products: 156 us -> none  [the longest x4 36.1 us: back_proj(): jnp.einsum('ne,de->nd', rows, weight, preferred_element_type=jnp.float32)]
    ppermute x30 -> x0, starting transfers between devices: 96.2 us -> none  [the longest x15 67.1 us: fwd_hop(): return lax.ppermute(carried + kv_total, 'sp', perm=fwd_perm)]
    add x31 -> x0, other arithmetic: 71.4 us -> none  [the longest x15 35 us: rev_hop(): return lax.ppermute(carried + qdo_total, 'sp', perm=rev_perm)]
    unnamed x51 -> x4, local copies, waits for them, and re-layouts: 47.2 us -> 5.59 us
    reshape x6 -> x0, local copies, waits for them, and re-layouts: 38.7 us -> none  [split_heads(): return tensor.reshape(n_blocks, BLOCK_LEN, n_heads, HEAD_DIM)]
  transfers between devices with their start and end apart: 31 -> 0, of which waited for: 31 -> 0; matrix products, arithmetic and copies ran while one was open for 3% -> 0% of each run, Pallas kernels for 0% -> 0%
where the time goes in v1:
time: 490 us; the launch traced here: 489 us
  Pallas kernels  483 us (99%)
  local copies, waits for them, and re-layouts  5.59 us (1%)
    pallas_call x1, Pallas kernels, local_layer(): pl.pallas_call(functools.partial(gather_kernel, n_seq), out_shape=(pltpu....  194 us
    pallas_call x1, Pallas kernels, local_layer(): pl.pallas_call(functools.partial(reduce_kernel, n_seq), out_shape=(jax.Sh...  193 us
    pallas_call x1, Pallas kernels, local_layer(): pl.pallas_call(functools.partial(attention_kernel, n_seq, scale), out_sha...  84.3 us
    pallas_call x1, Pallas kernels, local_layer(): pl.pallas_call(place_kernel, out_shape=(jax.ShapeDtypeStruct((dim, dim),...  12.1 us

profile of v1, /device:TPU:21, one launch (start us, length us, event | category | flops | bytes accessed | tf_op | source)
XLA Modules:
  0.0 489.4 jit_solution(16502788243637610728)
XLA Ops:
  0.6 84.3 %attention.1 = (bf16[2048,2304]{1,0:T(8,128)(2,1)}, bf16[2048,3840]{1,0:T(8,128)(2,1)}) custom-call(bf16[1024,1536]{1,0:T(8,128)(2,1)} %x.1, bf16[1024,1536]{1,0:T(8,128)(2,1)} %dy.1, bf16[1536,1536]{1,0:T(8,128)(2,1)} %wq.3, bf16[1536,1536]{1,0:T(8,128)(2,1)} %wk.3, bf16[1536,1536]{1,0:T(8,128)(2,1)} %wv.3, bf16[1536,1536]{1,0:T(8,128)(2,1)} %wo.3), custom_call_target="tpu_custom_call" | custom-call | tf_op jit(solution)/shard_map/attention/pallas_call | solution.py:459
  84.9 193.2 %reduce.1 = (f32[6,128,768]{2,1,0:T(8,128)}, bf16[4,1024,1536]{2,1,0:T(8,128)(2,1)}) custom-call(bf16[2048,2304]{1,0:T(8,128)(2,1)} %get-tuple-element.17.xo, bf16[2048,3840]{1,0:T(8,128)(2,1)} %get-tuple-element.18.ra), custom_call_target="tpu_custom_call" | custom-call | tf_op jit(solution)/shard_map/reduce/pallas_call | solution.py:475
  278.2 193.5 %gather.1 = (f32[2,48,128,768]{3,2,1,0:T(8,128)S(1)}, bf16[1024,1536]{1,0:T(8,128)(2,1)}, bf16[1024,1536]{1,0:T(8,128)(2,1)}) custom-call(f32[6,128,768]{2,1,0:T(8,128)} %get-tuple-element.19.red, bf16[4,1024,1536]{2,1,0:T(8,128)(2,1)} %get-tuple-element.20.own, bf16[1536,1536]{1,0:T(8,128)(2,1)} %wq.3, bf16[1536,1536]{1,0:T(8,128)(2,1)} %wk.3, ...), custom_call_target="tpu_custom_call" | custom-call | tf_op jit(solution)/shard_map/gather/pallas_call | solution.py:488
  471.7 12.1 %place.1 = (f32[1536,1536]{1,0:T(8,128)}, f32[1536,1536]{1,0:T(8,128)}, f32[1536,1536]{1,0:T(8,128)}, f32[1536,1536]{1,0:T(8,128)}) custom-call(f32[2,48,128,768]{3,2,1,0:T(8,128)S(1)} %get-tuple-element.23.both), custom_call_target="tpu_custom_call" | custom-call | tf_op jit(solution)/shard_map/place/pallas_call | solution.py:500
  483.8 0.0 copy-start
  483.8 3.9 copy.14
  487.8 0.0 copy-done
  487.8 1.7 copy.15
Async XLA Ops:
  483.8 3.9 copy-start

commit v2 on v1

v2 whole, which is shorter than its diff:
```python
import functools
import math
import jax
import jax.numpy as jnp
from jax import lax
from jax.experimental import pallas as pl
from jax.experimental.pallas import tpu as pltpu
from jax.sharding import PartitionSpec as P

HEAD_DIM = 128
BLOCK_LEN = 128
TILE = 128
ROWS = 256
MESH = pl.DeviceIdType.MESH
VMEM_LIMIT = 67_043_328
F32 = jnp.float32
BF16 = jnp.bfloat16


def dot_t(lhs, rhs):
    return lax.dot_general(lhs, rhs, (((0,), (0,)), ((), ())), preferred_element_type=F32)


def dot_nt(lhs, rhs):
    return lax.dot_general(lhs, rhs, (((1,), (1,)), ((), ())), preferred_element_type=F32)


def dot(lhs, rhs):
    return jnp.dot(lhs, rhs, preferred_element_type=F32)


def aligned(index, size):
    return pl.ds(pl.multiple_of(index * size, size), size)


def position(n_seq):
    me = lax.axis_index("sp")
    core, chip = lax.rem(me, 2), lax.div(me, 2)
    return core, chip, n_seq // 2, me + 1 - 2 * core


def send(src, dst, send_sem, recv_sem, target):
    return pltpu.make_async_remote_copy(src_ref=src, dst_ref=dst, send_sem=send_sem, recv_sem=recv_sem, device_id={"sp": target}, device_id_type=MESH)


def entry_barrier(targets):
    barrier = pltpu.get_barrier_semaphore()
    for target in targets:
        pl.semaphore_signal(barrier, inc=1, device_id={"sp": target}, device_id_type=MESH)
    pl.semaphore_wait(barrier, len(targets))


def ring(n_seq):
    core, chip, n_chips, peer = position(n_seq)
    me = lax.axis_index("sp")
    rank = (1 - core) * chip + core * lax.rem(n_chips - chip, n_chips)
    following = lax.rem(me + 2 - 4 * core + n_seq, n_seq)
    previous = lax.rem(me - 2 + 4 * core + n_seq, n_seq)
    return core, rank, n_chips, peer, following, previous


def attention_kernel(n_seq, scale, x, dy, wq, wk, wv, wo, red_out, own_out, xo, ra, w_s, q, do, grads, land, s_in, s_out, r_in, r_out, x_sems, w_sems, chain_sems, send_sems, recv_sems, own_sems, red_sems, credits):
    _, chip, _, _ = position(n_seq)
    core, rank, n_chips, peer, following, previous = ring(n_seq)
    me = lax.axis_index("sp")
    up, down = lax.rem(me + 2, n_seq), lax.rem(me + n_seq - 2, n_seq)
    n_rows, dim = x.shape
    all_rows, width = q.shape
    n_heads = width // HEAD_DIM
    n_blocks = all_rows // BLOCK_LEN
    n_slots = grads.shape[0]
    per_weight = dim // TILE
    early = 2 * per_weight // n_chips
    own_rows, peer_rows = aligned(core, n_rows), aligned(1 - core, n_rows)
    w_cols = aligned(core, width)
    k_col, v_col, a_row, b_row = width + dim, 2 * width + dim, 0, all_rows
    kv_slot, qdo_slot = 0, n_slots // 2

    entry_barrier((peer, up, down))
    x_part, dy_part = pl.ds(0, dim), pl.ds(width, dim)
    local, remote = [], []
    for index, (src, dst) in enumerate(((x, xo.at[own_rows, x_part]), (dy, ra.at[own_rows, dy_part]))):
        remote.append(send(src, dst, x_sems.at[index, 0], x_sems.at[index, 1], peer))
        local.append(pltpu.make_async_copy(src, dst, x_sems.at[index, 2]))
    w_loads = [pltpu.make_async_copy(weight.at[:, w_cols], w_s.at[pl.ds(index * dim, dim)], w_sems.at[index]) for index, weight in enumerate((wk, wv, wq))]
    for part in range(2):
        w_loads.append(pltpu.make_async_copy(wo.at[w_cols, pl.ds(part * width, width)], w_s.at[pl.ds(3 * dim + part * width, width)], w_sems.at[3 + part]))
    remote[0].start()
    local[0].start()
    for load in w_loads[:2]:
        load.start()
    remote[1].start()
    for load in w_loads[2:]:
        load.start()
    local[1].start()

    def weight(index, size):
        return w_s[pl.ds(index * size, size), :]

    def part_rows(half, step):
        return pl.ds(pl.multiple_of(half * n_rows + step * ROWS, ROWS), ROWS)

    def project_kv(half):
        @pl.loop(0, n_rows // ROWS)
        def _(step):
            rows = part_rows(half, step)
            ra[rows, pl.ds(k_col, width)] = dot(xo[rows, x_part], weight(0, dim)).astype(BF16)
            ra[rows, pl.ds(v_col, width)] = dot(xo[rows, x_part], weight(1, dim)).astype(BF16)

    local[0].wait()
    w_loads[0].wait()
    w_loads[1].wait()
    project_kv(core)
    remote[0].wait()
    project_kv(1 - core)

    def head(h, column=0):
        return pl.ds(column + h * HEAD_DIM, HEAD_DIM)

    def accumulate(left, right, slot, total, reverse):
        total[...] = jnp.zeros_like(total)

        @pl.loop(0, n_blocks)
        def _(step):
            block = (n_blocks - 1 - step) if reverse else step
            rows = aligned(block, BLOCK_LEN)
            for h in range(n_heads):
                running = total[h]
                grads[slot + block, :, head(h)] = running
                total[h] = running + dot_t(left(rows, h), right(rows, h))

    def q_of(rows, h):
        return q[rows, head(h)]

    def do_of(rows, h):
        return do[rows, head(h)]

    def k_of(rows, h):
        return ra[rows, head(h, k_col)]

    def v_of(rows, h):
        return ra[rows, head(h, v_col)]

    def chain_copy(which, h):
        src, dst, target = ((s_out, s_in, up), (r_out, r_in, down))[which]
        return send(src.at[h], dst.at[h], chain_sems.at[which, 0, h], chain_sems.at[which, 1, h], target)

    def chain_step(which, h):
        first, last = ((0, n_chips - 1), (n_chips - 1, 0))[which]
        src, dst = ((s_out, s_in), (r_out, r_in))[which]

        @pl.when(chip == first)
        def _():
            dst[h] = jnp.zeros_like(dst[h])

        @pl.when(chip != first)
        def _():
            chain_copy(which, h).wait_recv()
            src[h] = src[h] + dst[h]

        @pl.when(chip != last)
        def _():
            chain_copy(which, h).start()

    def chain_s(tick):
        @pl.when((tick >= 3 * chip) & (tick < 3 * chip + n_heads))
        def _():
            chain_step(0, tick - 3 * chip)

    accumulate(k_of, v_of, kv_slot, s_out, False)

    steps = n_rows // ROWS

    def project_qdo(half, first_tick):
        @pl.loop(0, steps)
        def _(step):
            chain_s(first_tick + step)
            rows = part_rows(half, step)
            q[rows, :] = dot(xo[rows, x_part], weight(2, dim)).astype(BF16)
            product = dot_nt(ra[rows, pl.ds(width, width)], weight(6, width))
            product += dot_nt(ra[rows, pl.ds(2 * width, width)], weight(7, width))
            do[rows, :] = product.astype(BF16)

    for load in w_loads[2:] + [local[1]]:
        load.wait()
    project_qdo(core, 0)
    remote[1].wait()
    project_qdo(1 - core, steps)

    causal = lax.broadcasted_iota(jnp.int32, (BLOCK_LEN, BLOCK_LEN), 0) >= lax.broadcasted_iota(jnp.int32, (BLOCK_LEN, BLOCK_LEN), 1)

    def block_scores(block):
        rows = aligned(block, BLOCK_LEN)
        a_rows = pl.ds(pl.multiple_of(a_row + block * BLOCK_LEN, BLOCK_LEN), BLOCK_LEN)
        b_rows = pl.ds(pl.multiple_of(b_row + block * BLOCK_LEN, BLOCK_LEN), BLOCK_LEN)
        for h in range(n_heads):
            w_s[a_rows, head(h)] = jnp.where(causal, dot_nt(q_of(rows, h), k_of(rows, h)), 0.0).astype(BF16)
            w_s[b_rows, head(h)] = jnp.where(causal, dot_nt(do_of(rows, h), v_of(rows, h)), 0.0).astype(BF16)

    @pl.loop(0, max(3 * (n_chips - 1) + n_heads - 2 * steps, n_blocks))
    def _(step):
        chain_s(2 * steps + step)

        @pl.when(step < n_blocks)
        def _():
            block_scores(step)

    def scores(block, h):
        a_rows = pl.ds(pl.multiple_of(a_row + block * BLOCK_LEN, BLOCK_LEN), BLOCK_LEN)
        b_rows = pl.ds(pl.multiple_of(b_row + block * BLOCK_LEN, BLOCK_LEN), BLOCK_LEN)
        return w_s[a_rows, head(h)], w_s[b_rows, head(h)]

    def both(left, right, top, bottom):
        out = dot(jnp.concatenate([left, right], axis=1), jnp.concatenate([top, bottom], axis=0))
        return (out * scale).astype(BF16)

    @pl.loop(0, n_blocks)
    def _(block):
        rows = aligned(block, BLOCK_LEN)
        for h in range(n_heads):
            a, b = scores(block, h)
            s = (s_in[h] + grads[kv_slot + block, :, head(h)]).astype(BF16)
            xo[rows, head(h, dim)] = both(a, q_of(rows, h), v_of(rows, h), s)
            ra[rows, head(h)] = both(b, do_of(rows, h), k_of(rows, h), s.T)

    def rev_block(block):
        rows = aligned(block, BLOCK_LEN)
        for h in range(n_heads):
            a, b = scores(block, h)
            r = (r_in[h] + grads[qdo_slot + block, :, head(h)]).astype(BF16)
            dk = both(b.T, v_of(rows, h), q_of(rows, h), r.T)
            dv = both(a.T, k_of(rows, h), do_of(rows, h), r)
            ra[rows, head(h, k_col)] = dk
            ra[rows, head(h, v_col)] = dv

    def credit(which):
        pl.semaphore_signal(credits.at[which], inc=1, device_id={"sp": previous}, device_id_type=MESH)

    def term(late, unit):
        inside, second = lax.rem(unit, per_weight), lax.div(unit, per_weight)
        if late:
            left, right = inside, 3 + second
        else:
            left = (1 - second) * inside + second * (per_weight + lax.div(inside, 2))
            right = second * (1 + lax.rem(inside, 2))
        return dot_t(xo[:, aligned(left, TILE)], ra[:, aligned(right, width)])

    def unit_of(step, piece):
        return lax.rem(rank - step + n_chips, n_chips) * early + piece

    def hop(late, step, piece):
        slot = grads.at[late * (n_slots // 2) + unit_of(step, piece)]
        sems = send_sems.at[late, step, piece], recv_sems.at[late, step, piece]
        return slot, sems

    def start_hop(late, step, piece, first):
        slot, sems = hop(late, step, piece)
        send(slot, land.at[late * early + piece] if first else slot, *sems, following).start()

    def run_ring(late, extra):
        offset = late * (n_slots // 2)

        @pl.loop(0, early)
        def _(piece):
            unit = unit_of(0, piece)
            grads[offset + unit] = term(late, unit)
            start_hop(late, 0, piece, True)

        @pl.loop(0, (n_chips - 1) * early)
        def _(index):
            step, piece = lax.div(index, early) + 1, lax.rem(index, early)
            unit = unit_of(step, piece)
            slot = offset + unit
            extra(index)
            mine = term(late, unit)

            @pl.when(step == 1)
            def _():
                place = land.at[late * early + piece]
                send(place, place, send_sems.at[late, 0, piece], recv_sems.at[late, 0, piece], following).wait_recv()
                grads[slot] = place[...] + mine

            @pl.when(step > 1)
            def _():
                place = grads.at[slot]
                send(place, place, send_sems.at[late, step - 1, piece], recv_sems.at[late, step - 1, piece], following).wait_recv()
                grads[slot] = grads[slot] + mine

            @pl.when(index == 0)
            def _():
                pl.semaphore_wait(credits.at[late], 1)

            @pl.when(step < n_chips - 1)
            def _():
                start_hop(late, step, piece, False)

            @pl.when(step == n_chips - 1)
            def _():
                pltpu.make_async_copy(grads.at[slot], red_out.at[late * early + piece], red_sems.at[late * early + piece]).start()

    share = n_blocks // 4

    def reverse_work(index):
        @pl.when(index == 0)
        def _():
            accumulate(q_of, do_of, qdo_slot, r_out, True)

        @pl.when(index == n_chips - chip)
        def _():
            for h in range(n_heads):
                chain_step(1, h)

        @pl.when((index > n_chips) & (index <= n_chips + 4))
        def _():
            @pl.loop(0, share)
            def _(part):
                rev_block((index - n_chips - 1) * share + part)

        @pl.when(index == n_chips + 4)
        def _():
            credit(1)

    credit(0)
    run_ring(0, reverse_work)

    copies = []
    for index, (src, column) in enumerate(((xo, dim), (ra, 0), (ra, k_col), (ra, v_col))):
        part = pl.ds(column, width)
        copies.append(pltpu.make_async_copy(src.at[own_rows, part], own_out.at[index, :, w_cols], own_sems.at[index, 0]))
        copies.append(send(src.at[peer_rows, part], own_out.at[index, :, w_cols], own_sems.at[index, 1], own_sems.at[index, 2], peer))
    for copy in copies:
        copy.start()

    run_ring(1, lambda index: None)

    for which, last in ((0, n_chips - 1), (1, 0)):
        @pl.when(chip != last)
        def _():
            for h in range(n_heads):
                chain_copy(which, h).wait_send()

    for late in range(2):
        @pl.loop(0, (n_chips - 1) * early)
        def _(index):
            step, piece = lax.div(index, early), lax.rem(index, early)
            slot, sems = hop(late, step, piece)
            send(slot, slot, *sems, following).wait_send()

    for copy in copies:
        copy.wait()
    for late in range(2):
        for piece in range(early):
            slot = late * (n_slots // 2) + lax.rem(rank + 1, n_chips) * early + piece
            pltpu.make_async_copy(grads.at[slot], red_out.at[late * early + piece], red_sems.at[late * early + piece]).wait()


def tile_slot(chunk, piece, early):
    return chunk * early + lax.rem(piece, early), lax.div(piece, early)


def gather_kernel(n_seq, red, own, wq, wk, wv, wo, rows_out, both_out, own_s, wo_s, w_s, own_sems, w_sems, send_sems, recv_sems, peer_sems):
    core, rank, n_chips, peer, following, previous = ring(n_seq)
    mine_out, peer_out = both_out.at[0], both_out.at[1]
    y_out, dx_out = rows_out.at[0], rows_out.at[1]
    n_slots, _, width = mine_out.shape
    dim = 2 * width
    early = 2 * (dim // TILE) // n_chips
    pieces = 2 * early
    n_rows = own.shape[1]
    unit_cols = wo_s.shape[2]
    n_units = dim // unit_cols
    row_blocks = n_rows // ROWS

    def slot_of(chunk, piece):
        unit, late = tile_slot(chunk, piece, early)
        return unit + late * (n_slots // 2)

    def held(step, piece):
        return slot_of(lax.rem(rank + 1 - step + n_chips, n_chips), piece)

    def w_loads(unit, buffer):
        part = aligned(unit, unit_cols)
        loads = [pltpu.make_async_copy(wo.at[:, part], wo_s.at[buffer], w_sems.at[buffer, 0])]
        for index, weight in enumerate((wq, wk, wv)):
            loads.append(pltpu.make_async_copy(weight.at[part], w_s.at[buffer, index], w_sems.at[buffer, 1 + index]))
        return loads

    own_load = pltpu.make_async_copy(own, own_s, own_sems.at[0])
    own_load.start()
    for unit in range(2):
        for load in w_loads(unit, unit):
            load.start()
    red_loads = [pltpu.make_async_copy(red.at[piece], mine_out.at[held(0, piece)], own_sems.at[1 + piece]) for piece in range(pieces)]
    for load in red_loads:
        load.start()

    entry_barrier((peer, following, previous))

    def to_next(step, piece):
        slot = held(step, piece)
        return send(mine_out.at[slot], mine_out.at[slot], send_sems.at[step, piece], recv_sems.at[step, piece], following)

    def arrival(step, piece):
        slot = held(step + 1, piece)
        return send(mine_out.at[slot], mine_out.at[slot], send_sems.at[step, piece], recv_sems.at[step, piece], following)

    def to_peer(step, piece):
        slot = held(step, piece)
        return send(mine_out.at[slot], peer_out.at[slot], peer_sems.at[0, step, piece], peer_sems.at[1, step, piece], peer)

    for piece in range(pieces):
        red_loads[piece].wait()
        to_next(0, piece).start()
        to_peer(0, piece).start()
    own_load.wait()

    def project(unit, block):
        buffer = lax.rem(unit, 2)

        @pl.when(block == 0)
        def _():
            for load in w_loads(unit, buffer):
                load.wait()

        rows, cols = aligned(block, ROWS), aligned(unit, unit_cols)
        y_out[rows, cols] = dot(own_s[0, rows, :], wo_s[buffer]).astype(BF16)
        total = dot_nt(own_s[1, rows, :], w_s[buffer, 0])
        total += dot_nt(own_s[2, rows, :], w_s[buffer, 1])
        total += dot_nt(own_s[3, rows, :], w_s[buffer, 2])
        dx_out[rows, cols] = total.astype(BF16)

        @pl.when((block == row_blocks - 1) & (unit + 2 < n_units))
        def _():
            for load in w_loads(unit + 2, buffer):
                load.start()

    @pl.loop(0, (n_chips - 1) * pieces)
    def _(index):
        step, piece = lax.div(index, pieces), lax.rem(index, pieces)

        @pl.when(index < n_units * row_blocks)
        def _():
            project(lax.div(index, row_blocks), lax.rem(index, row_blocks))

        arrival(step, piece).wait_recv()

        @pl.when(step < n_chips - 2)
        def _():
            to_next(step + 1, piece).start()

        to_peer(step + 1, piece).start()

    @pl.loop(0, n_chips * pieces)
    def _(index):
        step, piece = lax.div(index, pieces), lax.rem(index, pieces)

        @pl.when(step < n_chips - 1)
        def _():
            to_next(step, piece).wait_send()

        to_peer(step, piece).wait()


def place_kernel(results, both, y, dx, gq, gk, gv, go, sems):
    core = lax.rem(lax.axis_index("sp"), 2)
    _, n_slots, _, width = both.shape
    per_weight = n_slots // 4
    copies = [pltpu.make_async_copy(results.at[0], y, sems.at[2]), pltpu.make_async_copy(results.at[1], dx, sems.at[3])]
    for side, half in enumerate((core, 1 - core)):
        cols = aligned(half, width)
        for slot in range(n_slots):
            weight, inside = slot // per_weight, slot % per_weight
            if weight == 1:
                rows = pl.ds(pl.multiple_of(half * width + inside // 2 * TILE, TILE), TILE)
                dst = go.at[rows, pl.ds(inside % 2 * width, width)]
            else:
                dst = (gq, None, gk, gv)[weight].at[pl.ds(inside * TILE, TILE), cols]
            copies.append(pltpu.make_async_copy(both.at[side, slot], dst, sems.at[side]))
    for copy in copies:
        copy.start()
    for copy in copies:
        copy.wait()


def solution(mesh):
    n_seq = mesh.shape["sp"]
    n_chips = n_seq // 2
    row_spec = P(("dp", "sp"), None)
    grad_spec = P("dp", None)
    any_spec = pl.BlockSpec(memory_space=pl.ANY)
    vmem_spec = pl.BlockSpec(memory_space=pltpu.VMEM)
    dma = pltpu.SemaphoreType.DMA

    def params(collective_id, limit=VMEM_LIMIT):
        return pltpu.CompilerParams(collective_id=collective_id, has_side_effects=True, vmem_limit_bytes=limit)

    def local_layer(tokens, w_q, w_k, w_v, w_o, grad_y):
        n_rows, dim = tokens.shape
        width = dim // 2
        n_heads = width // HEAD_DIM
        rows = 2 * n_rows
        n_slots = 4 * (dim // TILE)
        pieces = n_slots // n_chips
        scale = 1.0 / math.sqrt(n_rows * n_seq * HEAD_DIM)
        state = (n_heads, HEAD_DIM, HEAD_DIM)

        red, own = pl.pallas_call(
            functools.partial(attention_kernel, n_seq, scale),
            out_shape=(jax.ShapeDtypeStruct((pieces, TILE, width), F32), jax.ShapeDtypeStruct((4, n_rows, dim), BF16)),
            in_specs=[any_spec] * 6,
            out_specs=(any_spec,) * 2,
            scratch_shapes=[pltpu.VMEM((rows, dim + width), BF16), pltpu.VMEM((rows, dim + 3 * width), BF16), pltpu.VMEM((4 * dim, width), BF16)]
            + [pltpu.VMEM((rows, width), BF16)] * 2
            + [pltpu.VMEM((n_slots, TILE, width), F32), pltpu.VMEM((pieces, TILE, width), F32)]
            + [pltpu.VMEM(state, F32)] * 4
            + [dma((2, 3)), dma((5,)), dma((2, 2, n_heads))]
            + [dma((2, n_chips - 1, pieces // 2))] * 2
            + [dma((4, 3)), dma((pieces,)), pltpu.SemaphoreType.REGULAR((2,))],
            compiler_params=params(0),
            name="attention",
        )(tokens, grad_y, w_q, w_k, w_v, w_o)

        unit_cols = min(256, dim // 2)
        halves = (2, n_slots, TILE, width)
        room = VMEM_LIMIT - math.prod(halves) * 4 - 4 * n_rows * dim - (1 << 20)
        results = pl.pallas_call(
            functools.partial(gather_kernel, n_seq),
            out_shape=(pltpu.VMEM((2, n_rows, dim), BF16), pltpu.VMEM(halves, F32)),
            in_specs=[any_spec] * 6,
            out_specs=(vmem_spec,) * 2,
            scratch_shapes=[pltpu.VMEM((4, n_rows, dim), BF16), pltpu.VMEM((2, dim, unit_cols), BF16), pltpu.VMEM((2, 3, unit_cols, dim), BF16)]
            + [dma((1 + pieces,)), dma((2, 4)), dma((n_chips - 1, pieces)), dma((n_chips - 1, pieces)), dma((2, n_chips, pieces))],
            compiler_params=params(1, room),
            name="gather",
        )(red, own, w_q, w_k, w_v, w_o)

        return pl.pallas_call(
            place_kernel,
            out_shape=(jax.ShapeDtypeStruct((n_rows, dim), BF16),) * 2 + (jax.ShapeDtypeStruct((dim, dim), F32),) * 4,
            in_specs=[vmem_spec] * 2,
            out_specs=(any_spec,) * 6,
            scratch_shapes=[dma((4,))],
            compiler_params=pltpu.CompilerParams(vmem_limit_bytes=1 << 20),
            name="place",
        )(*results)

    return jax.shard_map(local_layer, mesh=mesh, in_specs=(row_spec, P(), P(), P(), P(), row_spec), out_specs=(row_spec, row_spec, grad_spec, grad_spec, grad_spec, grad_spec), check_vma=False)
```

time: 490 us -> 452 us (0.922)
  Pallas kernels: 483 us -> 451 us
  local copies, waits for them, and re-layouts: 5.59 us -> 0 us
    pallas_call x2 -> x1, Pallas kernels: 205 us -> 14.1 us  [local_layer(): pl.pallas_call(place_kernel, out_shape=(jax.ShapeDtypeStruct((n_rows, dim...]
    pallas_call x1, Pallas kernels: 84.3 us -> 248 us  [local_layer(): pl.pallas_call(functools.partial(attention_kernel, n_seq, scale), out_sha...]
    unnamed x4 -> x0, local copies, waits for them, and re-layouts: 5.59 us -> none
where the time goes in v2:
time: 452 us
  Pallas kernels  451 us (100%)
    pallas_call x1, Pallas kernels, local_layer(): pl.pallas_call(functools.partial(attention_kernel, n_seq, scale), out_sha...  248 us
    pallas_call x1, Pallas kernels, local_layer(): pl.pallas_call(functools.partial(gather_kernel, n_seq), out_shape=(pltpu....  189 us
    pallas_call x1, Pallas kernels, local_layer(): pl.pallas_call(place_kernel, out_shape=(jax.ShapeDtypeStruct((n_rows, dim...  14.1 us

profile of v2, /device:TPU:21, one launch (start us, length us, event | category | flops | bytes accessed | tf_op | source)
XLA Modules:
  0.0 451.8 jit_solution(6129492230732436000)
XLA Ops:
  0.6 248.4 %attention.1 = (f32[6,128,768]{2,1,0:T(8,128)}, bf16[4,1024,1536]{2,1,0:T(8,128)(2,1)}) custom-call(bf16[1024,1536]{1,0:T(8,128)(2,1)} %x.1, bf16[1024,1536]{1,0:T(8,128)(2,1)} %dy.1, bf16[1536,1536]{1,0:T(8,128)(2,1)} %wq.3, bf16[1536,1536]{1,0:T(8,128)(2,1)} %wk.3, bf16[1536,1536]{1,0:T(8,128)(2,1)} %wv.3, bf16[1536,1536]{1,0:T(8,128)(2,1)} %wo.3), custom_call_target="tpu_custom_call" | custom-call | tf_op jit(solution)/shard_map/attention/pallas_call | solution.py:507
  249.1 188.7 %gather.1 = (bf16[2,1024,1536]{2,1,0:T(8,128)(2,1)S(1)}, f32[2,48,128,768]{3,2,1,0:T(8,128)S(1)}) custom-call(f32[6,128,768]{2,1,0:T(8,128)} %get-tuple-element.10.red, bf16[4,1024,1536]{2,1,0:T(8,128)(2,1)} %get-tuple-element.11.own, bf16[1536,1536]{1,0:T(8,128)(2,1)} %wq.3, bf16[1536,1536]{1,0:T(8,128)(2,1)} %wk.3, bf16[1536,1536]{1,0:T(8,128)(2,1)} %wv.3, ...), custom_call_target="tpu_custom_call" | custom-call | tf_op jit(solution)/shard_map/gather/pallas_call | solution.py:526
  437.8 14.1 %place.1 = (bf16[1024,1536]{1,0:T(8,128)(2,1)}, bf16[1024,1536]{1,0:T(8,128)(2,1)}, f32[1536,1536]{1,0:T(8,128)}, f32[1536,1536]{1,0:T(8,128)}, f32[1536,1536]{1,0:T(8,128)}, /*index=5*/f32[1536,1536]{1,0:T(8,128)}) custom-call(bf16[2,1024,1536]{2,1,0:T(8,128)(2,1)S(1)} %get-tuple-element.12.results, f32[2,48,128,768]{3,2,1,0:T(8,128)S(1)} %get-tuple-element.13.both), custom_call_target="tpu_custom_call" | custom-call | tf_op jit(solution)/shard_map/place/pallas_call | solution.py:537

commit v3 on v2

--- a/solution.py
+++ b/solution.py
@@ -59,11 +59,12 @@
     return core, rank, n_chips, peer, following, previous
 
 
-def attention_kernel(n_seq, scale, x, dy, wq, wk, wv, wo, red_out, own_out, xo, ra, w_s, q, do, grads, land, s_in, s_out, r_in, r_out, x_sems, w_sems, chain_sems, send_sems, recv_sems, own_sems, red_sems, credits):
+def attention_kernel(n_seq, scale, x, dy, wq, wk, wv, wo, own_out, red_out, xo, ra, w_s, q, do, grads, land, s_in, s_out, s_even, s_pair, r_in, r_out, x_sems, w_sems, chain_sems, send_sems, recv_sems, own_sems, red_sems, credits):
     _, chip, _, _ = position(n_seq)
     core, rank, n_chips, peer, following, previous = ring(n_seq)
     me = lax.axis_index("sp")
     up, down = lax.rem(me + 2, n_seq), lax.rem(me + n_seq - 2, n_seq)
+    up_two, down_two = lax.rem(me + 4, n_seq), lax.rem(me + n_seq - 4, n_seq)
     n_rows, dim = x.shape
     all_rows, width = q.shape
     n_heads = width // HEAD_DIM
@@ -76,7 +77,7 @@
     k_col, v_col, a_row, b_row = width + dim, 2 * width + dim, 0, all_rows
     kv_slot, qdo_slot = 0, n_slots // 2
 
-    entry_barrier((peer, up, down))
+    entry_barrier((peer, up, down, up_two, down_two))
     x_part, dy_part = pl.ds(0, dim), pl.ds(width, dim)
     local, remote = [], []
     for index, (src, dst) in enumerate(((x, xo.at[own_rows, x_part]), (dy, ra.at[own_rows, dy_part]))):
@@ -115,15 +116,16 @@
     project_kv(1 - core)
 
     def head(h, column=0):
-        return pl.ds(column + h * HEAD_DIM, HEAD_DIM)
-
-    def accumulate(left, right, slot, total, reverse):
+        return pl.ds(pl.multiple_of(column + h * HEAD_DIM, HEAD_DIM), HEAD_DIM)
+
+    def accumulate(left, right, slot, total, reverse, extra):
         total[...] = jnp.zeros_like(total)
 
         @pl.loop(0, n_blocks)
         def _(step):
             block = (n_blocks - 1 - step) if reverse else step
             rows = aligned(block, BLOCK_LEN)
+            extra(step)
             for h in range(n_heads):
                 running = total[h]
                 grads[slot + block, :, head(h)] = running
@@ -141,35 +143,73 @@
     def v_of(rows, h):
         return ra[rows, head(h, v_col)]
 
+    odd = lax.rem(chip, 2)
+    EVEN, PAIR, HAND, REV = range(4)
+
     def chain_copy(which, h):
-        src, dst, target = ((s_out, s_in, up), (r_out, r_in, down))[which]
+        src, dst, target = ((s_out, s_even, up), (s_out, s_pair, up_two), (s_pair, s_in, down), (r_out, r_in, down))[which]
         return send(src.at[h], dst.at[h], chain_sems.at[which, 0, h], chain_sems.at[which, 1, h], target)
 
-    def chain_step(which, h):
-        first, last = ((0, n_chips - 1), (n_chips - 1, 0))[which]
-        src, dst = ((s_out, s_in), (r_out, r_in))[which]
-
-        @pl.when(chip == first)
-        def _():
-            dst[h] = jnp.zeros_like(dst[h])
-
-        @pl.when(chip != first)
-        def _():
-            chain_copy(which, h).wait_recv()
-            src[h] = src[h] + dst[h]
-
-        @pl.when(chip != last)
-        def _():
-            chain_copy(which, h).start()
+    def start_s():
+        @pl.when(odd == 0)
+        def _():
+            for h in range(n_heads):
+                chain_copy(EVEN, h).start()
+
+    def odd_s(h):
+        chain_copy(EVEN, h).wait_recv()
+
+        @pl.when(chip == 1)
+        def _():
+            s_in[h] = s_even[h]
+
+        @pl.when(chip != 1)
+        def _():
+            chain_copy(PAIR, h).wait_recv()
+            chain_copy(HAND, h).start()
+            s_in[h] = s_pair[h] + s_even[h]
+
+        @pl.when(chip + 2 < n_chips)
+        def _():
+            s_out[h] = s_out[h] + s_in[h]
+            chain_copy(PAIR, h).start()
+
+    def even_s(h):
+        @pl.when(chip == 0)
+        def _():
+            s_in[h] = jnp.zeros_like(s_in[h])
+
+        @pl.when(chip != 0)
+        def _():
+            chain_copy(HAND, h).wait_recv()
+
+    def chain_r(h):
+        @pl.when(chip == n_chips - 1)
+        def _():
+            r_in[h] = jnp.zeros_like(r_in[h])
+
+        @pl.when(chip != n_chips - 1)
+        def _():
+            chain_copy(REV, h).wait_recv()
+            r_out[h] = r_out[h] + r_in[h]
+
+        @pl.when(chip != 0)
+        def _():
+            chain_copy(REV, h).start()
+
+    steps = n_rows // ROWS
+    due = 3 + lax.div(7 * lax.div(chip, 2), 2)
+    stride_r, stride_scores = n_blocks // 2, -(-n_blocks // 3)
+    tick_r, tick_scores = 2 * steps, 2 * steps + 2
+    last_tick = tick_scores + -(-n_blocks // stride_scores)
 
     def chain_s(tick):
-        @pl.when((tick >= 3 * chip) & (tick < 3 * chip + n_heads))
-        def _():
-            chain_step(0, tick - 3 * chip)
-
-    accumulate(k_of, v_of, kv_slot, s_out, False)
-
-    steps = n_rows // ROWS
+        @pl.when((odd == 1) & (tick >= due) & (tick < due + n_heads))
+        def _():
+            odd_s(tick - due)
+
+    accumulate(k_of, v_of, kv_slot, s_out, False, lambda step: None)
+    start_s()
 
     def project_qdo(half, first_tick):
         @pl.loop(0, steps)
@@ -197,13 +237,27 @@
             w_s[a_rows, head(h)] = jnp.where(causal, dot_nt(q_of(rows, h), k_of(rows, h)), 0.0).astype(BF16)
             w_s[b_rows, head(h)] = jnp.where(causal, dot_nt(do_of(rows, h), v_of(rows, h)), 0.0).astype(BF16)
 
-    @pl.loop(0, max(3 * (n_chips - 1) + n_heads - 2 * steps, n_blocks))
-    def _(step):
-        chain_s(2 * steps + step)
-
-        @pl.when(step < n_blocks)
-        def _():
-            block_scores(step)
+    def spread(first_tick, stride):
+        def extra(step):
+            @pl.when(lax.rem(step, stride) == 0)
+            def _():
+                chain_s(first_tick + lax.div(step, stride))
+
+        return extra
+
+    accumulate(q_of, do_of, qdo_slot, r_out, True, spread(tick_r, stride_r))
+
+    @pl.when(chip == n_chips - 1)
+    def _():
+        for h in range(n_heads):
+            chain_r(h)
+
+    score_ticks = spread(tick_scores, stride_scores)
+
+    @pl.loop(0, n_blocks)
+    def _(block):
+        score_ticks(block)
+        block_scores(block)
 
     def scores(block, h):
         a_rows = pl.ds(pl.multiple_of(a_row + block * BLOCK_LEN, BLOCK_LEN), BLOCK_LEN)
@@ -214,14 +268,31 @@
         out = dot(jnp.concatenate([left, right], axis=1), jnp.concatenate([top, bottom], axis=0))
         return (out * scale).astype(BF16)
 
-    @pl.loop(0, n_blocks)
-    def _(block):
-        rows = aligned(block, BLOCK_LEN)
-        for h in range(n_heads):
-            a, b = scores(block, h)
-            s = (s_in[h] + grads[kv_slot + block, :, head(h)]).astype(BF16)
-            xo[rows, head(h, dim)] = both(a, q_of(rows, h), v_of(rows, h), s)
-            ra[rows, head(h)] = both(b, do_of(rows, h), k_of(rows, h), s.T)
+    group = 4
+
+    @pl.loop(0, n_heads)
+    def _(h):
+        @pl.when(chip == n_chips - 2)
+        def _():
+            chain_r(h)
+
+        @pl.when(odd == 0)
+        def _():
+            even_s(h)
+
+        @pl.when((odd == 1) & (due + h >= last_tick))
+        def _():
+            odd_s(h)
+
+        @pl.loop(0, n_blocks // group)
+        def _(part):
+            for inner in range(group):
+                block = part * group + inner
+                rows = aligned(block, BLOCK_LEN)
+                a, b = scores(block, h)
+                s = (s_in[h] + grads[kv_slot + block, :, head(h)]).astype(BF16)
+                xo[rows, head(h, dim)] = both(a, q_of(rows, h), v_of(rows, h), s)
+                ra[rows, head(h)] = both(b, do_of(rows, h), k_of(rows, h), s.T)
 
     def rev_block(block):
         rows = aligned(block, BLOCK_LEN)
@@ -301,14 +372,10 @@
     share = n_blocks // 4
 
     def reverse_work(index):
-        @pl.when(index == 0)
-        def _():
-            accumulate(q_of, do_of, qdo_slot, r_out, True)
-
-        @pl.when(index == n_chips - chip)
+        @pl.when(((index == n_chips // 2 - chip) | ((index == 0) & (chip > n_chips // 2))) & (chip < n_chips - 2))
         def _():
             for h in range(n_heads):
-                chain_step(1, h)
+                chain_r(h)
 
         @pl.when((index > n_chips) & (index <= n_chips + 4))
         def _():
@@ -333,8 +400,9 @@
 
     run_ring(1, lambda index: None)
 
-    for which, last in ((0, n_chips - 1), (1, 0)):
-        @pl.when(chip != last)
+    sent = ((EVEN, odd == 0), (PAIR, (odd == 1) & (chip + 2 < n_chips)), (HAND, (odd == 1) & (chip > 1)), (REV, chip > 0))
+    for which, sends in sent:
+        @pl.when(sends)
         def _():
             for h in range(n_heads):
                 chain_copy(which, h).wait_send()
@@ -504,16 +572,16 @@
         scale = 1.0 / math.sqrt(n_rows * n_seq * HEAD_DIM)
         state = (n_heads, HEAD_DIM, HEAD_DIM)
 
-        red, own = pl.pallas_call(
+        own, red = pl.pallas_call(
             functools.partial(attention_kernel, n_seq, scale),
-            out_shape=(jax.ShapeDtypeStruct((pieces, TILE, width), F32), jax.ShapeDtypeStruct((4, n_rows, dim), BF16)),
+            out_shape=(jax.ShapeDtypeStruct((4, n_rows, dim), BF16), jax.ShapeDtypeStruct((pieces, TILE, width), F32)),
             in_specs=[any_spec] * 6,
             out_specs=(any_spec,) * 2,
             scratch_shapes=[pltpu.VMEM((rows, dim + width), BF16), pltpu.VMEM((rows, dim + 3 * width), BF16), pltpu.VMEM((4 * dim, width), BF16)]
             + [pltpu.VMEM((rows, width), BF16)] * 2
             + [pltpu.VMEM((n_slots, TILE, width), F32), pltpu.VMEM((pieces, TILE, width), F32)]
-            + [pltpu.VMEM(state, F32)] * 4
-            + [dma((2, 3)), dma((5,)), dma((2, 2, n_heads))]
+            + [pltpu.VMEM(state, F32)] * 6
+            + [dma((2, 3)), dma((5,)), dma((4, 2, n_heads))]
             + [dma((2, n_chips - 1, pieces // 2))] * 2
             + [dma((4, 3)), dma((pieces,)), pltpu.SemaphoreType.REGULAR((2,))],
             compiler_params=params(0),

time: 452 us -> 463 us (1.024)
  Pallas kernels: 451 us -> 462 us
    pallas_call x1, Pallas kernels: 248 us -> 259 us  [local_layer(): pl.pallas_call(functools.partial(attention_kernel, n_seq, scale), out_sha...]
where the time goes in v3:
time: 463 us; the launch traced here: 462 us
  Pallas kernels  462 us (100%)
    pallas_call x1, Pallas kernels, local_layer(): pl.pallas_call(functools.partial(attention_kernel, n_seq, scale), out_sha...  259 us
    pallas_call x1, Pallas kernels, local_layer(): pl.pallas_call(functools.partial(gather_kernel, n_seq), out_shape=(pltpu....  189 us
    pallas_call x1, Pallas kernels, local_layer(): pl.pallas_call(place_kernel, out_shape=(jax.ShapeDtypeStruct((n_rows, dim...  14.1 us

profile of v3, /device:TPU:21, one launch (start us, length us, event | category | flops | bytes accessed | tf_op | source)
XLA Modules:
  0.0 462.5 jit_solution(16870679271694487114)
XLA Ops:
  0.6 259.0 %attention.1 = (bf16[4,1024,1536]{2,1,0:T(8,128)(2,1)}, f32[6,128,768]{2,1,0:T(8,128)}) custom-call(bf16[1024,1536]{1,0:T(8,128)(2,1)} %x.1, bf16[1024,1536]{1,0:T(8,128)(2,1)} %dy.1, bf16[1536,1536]{1,0:T(8,128)(2,1)} %wq.3, bf16[1536,1536]{1,0:T(8,128)(2,1)} %wk.3, bf16[1536,1536]{1,0:T(8,128)(2,1)} %wv.3, bf16[1536,1536]{1,0:T(8,128)(2,1)} %wo.3), custom_call_target="tpu_custom_call" | custom-call | tf_op jit(solution)/shard_map/attention/pallas_call | solution.py:575
  259.6 188.8 %gather.1 = (bf16[2,1024,1536]{2,1,0:T(8,128)(2,1)S(1)}, f32[2,48,128,768]{3,2,1,0:T(8,128)S(1)}) custom-call(f32[6,128,768]{2,1,0:T(8,128)} %get-tuple-element.10.red, bf16[4,1024,1536]{2,1,0:T(8,128)(2,1)} %get-tuple-element.11.own, bf16[1536,1536]{1,0:T(8,128)(2,1)} %wq.3, bf16[1536,1536]{1,0:T(8,128)(2,1)} %wk.3, bf16[1536,1536]{1,0:T(8,128)(2,1)} %wv.3, ...), custom_call_target="tpu_custom_call" | custom-call | tf_op jit(solution)/shard_map/gather/pallas_call | solution.py:594
  448.4 14.1 %place.1 = (bf16[1024,1536]{1,0:T(8,128)(2,1)}, bf16[1024,1536]{1,0:T(8,128)(2,1)}, f32[1536,1536]{1,0:T(8,128)}, f32[1536,1536]{1,0:T(8,128)}, f32[1536,1536]{1,0:T(8,128)}, /*index=5*/f32[1536,1536]{1,0:T(8,128)}) custom-call(bf16[2,1024,1536]{2,1,0:T(8,128)(2,1)S(1)} %get-tuple-element.12.results, f32[2,48,128,768]{3,2,1,0:T(8,128)S(1)} %get-tuple-element.13.both), custom_call_target="tpu_custom_call" | custom-call | tf_op jit(solution)/shard_map/place/pallas_call | solution.py:605

commit v4 on v3

--- a/solution.py
+++ b/solution.py
@@ -247,11 +247,6 @@
 
     accumulate(q_of, do_of, qdo_slot, r_out, True, spread(tick_r, stride_r))
 
-    @pl.when(chip == n_chips - 1)
-    def _():
-        for h in range(n_heads):
-            chain_r(h)
-
     score_ticks = spread(tick_scores, stride_scores)
 
     @pl.loop(0, n_blocks)
@@ -272,10 +267,6 @@
 
     @pl.loop(0, n_heads)
     def _(h):
-        @pl.when(chip == n_chips - 2)
-        def _():
-            chain_r(h)
-
         @pl.when(odd == 0)
         def _():
             even_s(h)
@@ -294,15 +285,18 @@
                 xo[rows, head(h, dim)] = both(a, q_of(rows, h), v_of(rows, h), s)
                 ra[rows, head(h)] = both(b, do_of(rows, h), k_of(rows, h), s.T)
 
-    def rev_block(block):
-        rows = aligned(block, BLOCK_LEN)
-        for h in range(n_heads):
-            a, b = scores(block, h)
-            r = (r_in[h] + grads[qdo_slot + block, :, head(h)]).astype(BF16)
-            dk = both(b.T, v_of(rows, h), q_of(rows, h), r.T)
-            dv = both(a.T, k_of(rows, h), do_of(rows, h), r)
-            ra[rows, head(h, k_col)] = dk
-            ra[rows, head(h, v_col)] = dv
+    def rev_head(h):
+        @pl.loop(0, n_blocks // group)
+        def _(part):
+            for inner in range(group):
+                block = part * group + inner
+                rows = aligned(block, BLOCK_LEN)
+                a, b = scores(block, h)
+                r = (r_in[h] + grads[qdo_slot + block, :, head(h)]).astype(BF16)
+                dk = both(b.T, v_of(rows, h), q_of(rows, h), r.T)
+                dv = both(a.T, k_of(rows, h), do_of(rows, h), r)
+                ra[rows, head(h, k_col)] = dk
+                ra[rows, head(h, v_col)] = dv
 
     def credit(which):
         pl.semaphore_signal(credits.at[which], inc=1, device_id={"sp": previous}, device_id_type=MESH)
@@ -369,21 +363,16 @@
             def _():
                 pltpu.make_async_copy(grads.at[slot], red_out.at[late * early + piece], red_sems.at[late * early + piece]).start()
 
-    share = n_blocks // 4
+    stride = ((n_chips - 1) * early - n_heads) // (n_chips - 1)
+    rev_start = stride * (n_chips - 1 - chip)
 
     def reverse_work(index):
-        @pl.when(((index == n_chips // 2 - chip) | ((index == 0) & (chip > n_chips // 2))) & (chip < n_chips - 2))
-        def _():
-            for h in range(n_heads):
-                chain_r(h)
-
-        @pl.when((index > n_chips) & (index <= n_chips + 4))
-        def _():
-            @pl.loop(0, share)
-            def _(part):
-                rev_block((index - n_chips - 1) * share + part)
-
-        @pl.when(index == n_chips + 4)
+        @pl.when((index >= rev_start) & (index < rev_start + n_heads))
+        def _():
+            chain_r(index - rev_start)
+            rev_head(index - rev_start)
+
+        @pl.when(index == rev_start + n_heads - 1)
         def _():
             credit(1)
 

time: 463 us -> 463 us (level)
  no operation moved by 1% of the time
where the time goes in v4:
time: 463 us; the launch traced here: 461 us
  Pallas kernels  461 us (100%)
    pallas_call x1, Pallas kernels, local_layer(): pl.pallas_call(functools.partial(attention_kernel, n_seq, scale), out_sha...  259 us
    pallas_call x1, Pallas kernels, local_layer(): pl.pallas_call(functools.partial(gather_kernel, n_seq), out_shape=(pltpu....  188 us
    pallas_call x1, Pallas kernels, local_layer(): pl.pallas_call(place_kernel, out_shape=(jax.ShapeDtypeStruct((n_rows, dim...  14.1 us

profile of v4, /device:TPU:21, one launch (start us, length us, event | category | flops | bytes accessed | tf_op | source)
XLA Modules:
  0.0 461.4 jit_solution(18285889581139603365)
XLA Ops:
  0.6 258.7 %attention.1 = (bf16[4,1024,1536]{2,1,0:T(8,128)(2,1)}, f32[6,128,768]{2,1,0:T(8,128)}) custom-call(bf16[1024,1536]{1,0:T(8,128)(2,1)} %x.1, bf16[1024,1536]{1,0:T(8,128)(2,1)} %dy.1, bf16[1536,1536]{1,0:T(8,128)(2,1)} %wq.3, bf16[1536,1536]{1,0:T(8,128)(2,1)} %wk.3, bf16[1536,1536]{1,0:T(8,128)(2,1)} %wv.3, bf16[1536,1536]{1,0:T(8,128)(2,1)} %wo.3), custom_call_target="tpu_custom_call" | custom-call | tf_op jit(solution)/shard_map/attention/pallas_call | solution.py:564
  259.4 187.9 %gather.1 = (bf16[2,1024,1536]{2,1,0:T(8,128)(2,1)S(1)}, f32[2,48,128,768]{3,2,1,0:T(8,128)S(1)}) custom-call(f32[6,128,768]{2,1,0:T(8,128)} %get-tuple-element.10.red, bf16[4,1024,1536]{2,1,0:T(8,128)(2,1)} %get-tuple-element.11.own, bf16[1536,1536]{1,0:T(8,128)(2,1)} %wq.3, bf16[1536,1536]{1,0:T(8,128)(2,1)} %wk.3, bf16[1536,1536]{1,0:T(8,128)(2,1)} %wv.3, ...), custom_call_target="tpu_custom_call" | custom-call | tf_op jit(solution)/shard_map/gather/pallas_call | solution.py:583
  447.3 14.1 %place.1 = (bf16[1024,1536]{1,0:T(8,128)(2,1)}, bf16[1024,1536]{1,0:T(8,128)(2,1)}, f32[1536,1536]{1,0:T(8,128)}, f32[1536,1536]{1,0:T(8,128)}, f32[1536,1536]{1,0:T(8,128)}, /*index=5*/f32[1536,1536]{1,0:T(8,128)}) custom-call(bf16[2,1024,1536]{2,1,0:T(8,128)(2,1)S(1)} %get-tuple-element.12.results, f32[2,48,128,768]{3,2,1,0:T(8,128)S(1)} %get-tuple-element.13.both), custom_call_target="tpu_custom_call" | custom-call | tf_op jit(solution)/shard_map/place/pallas_call | solution.py:594

commit v5 on v2

--- a/solution.py
+++ b/solution.py
@@ -11,6 +11,7 @@
 BLOCK_LEN = 128
 TILE = 128
 ROWS = 256
+PARTS = 2
 MESH = pl.DeviceIdType.MESH
 VMEM_LIMIT = 67_043_328
 F32 = jnp.float32
@@ -115,7 +116,11 @@
     project_kv(1 - core)
 
     def head(h, column=0):
-        return pl.ds(column + h * HEAD_DIM, HEAD_DIM)
+        start = column + h * HEAD_DIM
+        return pl.ds(start if isinstance(h, int) else pl.multiple_of(start, HEAD_DIM), HEAD_DIM)
+
+    def state_of(ref, h):
+        return ref[pl.ds(h * PARTS, PARTS)].reshape(HEAD_DIM, HEAD_DIM)
 
     def accumulate(left, right, slot, total, reverse):
         total[...] = jnp.zeros_like(total)
@@ -125,9 +130,9 @@
             block = (n_blocks - 1 - step) if reverse else step
             rows = aligned(block, BLOCK_LEN)
             for h in range(n_heads):
-                running = total[h]
+                running = state_of(total, h)
                 grads[slot + block, :, head(h)] = running
-                total[h] = running + dot_t(left(rows, h), right(rows, h))
+                total[pl.ds(h * PARTS, PARTS)] = (running + dot_t(left(rows, h), right(rows, h))).reshape(PARTS, HEAD_DIM // PARTS, HEAD_DIM)
 
     def q_of(rows, h):
         return q[rows, head(h)]
@@ -141,35 +146,39 @@
     def v_of(rows, h):
         return ra[rows, head(h, v_col)]
 
-    def chain_copy(which, h):
+    def chain_copy(which, unit):
         src, dst, target = ((s_out, s_in, up), (r_out, r_in, down))[which]
-        return send(src.at[h], dst.at[h], chain_sems.at[which, 0, h], chain_sems.at[which, 1, h], target)
+        return send(src.at[unit], dst.at[unit], chain_sems.at[which, 0, unit], chain_sems.at[which, 1, unit], target)
 
     def chain_step(which, h):
         first, last = ((0, n_chips - 1), (n_chips - 1, 0))[which]
         src, dst = ((s_out, s_in), (r_out, r_in))[which]
-
-        @pl.when(chip == first)
-        def _():
-            dst[h] = jnp.zeros_like(dst[h])
-
-        @pl.when(chip != first)
-        def _():
-            chain_copy(which, h).wait_recv()
-            src[h] = src[h] + dst[h]
-
-        @pl.when(chip != last)
-        def _():
-            chain_copy(which, h).start()
+        for part in range(PARTS):
+            unit = h * PARTS + part
+
+            @pl.when(chip == first)
+            def _():
+                dst[unit] = jnp.zeros_like(dst[unit])
+
+            @pl.when(chip != first)
+            def _():
+                chain_copy(which, unit).wait_recv()
+                src[unit] = src[unit] + dst[unit]
+
+            @pl.when(chip != last)
+            def _():
+                chain_copy(which, unit).start()
+
+    steps = n_rows // ROWS
+    stride = n_blocks // 4
+    due, last_tick = lax.div(5 * chip, 2), 2 * steps + 4
 
     def chain_s(tick):
-        @pl.when((tick >= 3 * chip) & (tick < 3 * chip + n_heads))
-        def _():
-            chain_step(0, tick - 3 * chip)
+        @pl.when((tick >= due) & (tick < due + n_heads))
+        def _():
+            chain_step(0, tick - due)
 
     accumulate(k_of, v_of, kv_slot, s_out, False)
-
-    steps = n_rows // ROWS
 
     def project_qdo(half, first_tick):
         @pl.loop(0, steps)
@@ -197,13 +206,13 @@
             w_s[a_rows, head(h)] = jnp.where(causal, dot_nt(q_of(rows, h), k_of(rows, h)), 0.0).astype(BF16)
             w_s[b_rows, head(h)] = jnp.where(causal, dot_nt(do_of(rows, h), v_of(rows, h)), 0.0).astype(BF16)
 
-    @pl.loop(0, max(3 * (n_chips - 1) + n_heads - 2 * steps, n_blocks))
-    def _(step):
-        chain_s(2 * steps + step)
-
-        @pl.when(step < n_blocks)
-        def _():
-            block_scores(step)
+    @pl.loop(0, n_blocks)
+    def _(block):
+        @pl.when(lax.rem(block, stride) == 0)
+        def _():
+            chain_s(2 * steps + lax.div(block, stride))
+
+        block_scores(block)
 
     def scores(block, h):
         a_rows = pl.ds(pl.multiple_of(a_row + block * BLOCK_LEN, BLOCK_LEN), BLOCK_LEN)
@@ -214,24 +223,40 @@
         out = dot(jnp.concatenate([left, right], axis=1), jnp.concatenate([top, bottom], axis=0))
         return (out * scale).astype(BF16)
 
-    @pl.loop(0, n_blocks)
-    def _(block):
-        rows = aligned(block, BLOCK_LEN)
-        for h in range(n_heads):
-            a, b = scores(block, h)
-            s = (s_in[h] + grads[kv_slot + block, :, head(h)]).astype(BF16)
-            xo[rows, head(h, dim)] = both(a, q_of(rows, h), v_of(rows, h), s)
-            ra[rows, head(h)] = both(b, do_of(rows, h), k_of(rows, h), s.T)
-
-    def rev_block(block):
-        rows = aligned(block, BLOCK_LEN)
-        for h in range(n_heads):
-            a, b = scores(block, h)
-            r = (r_in[h] + grads[qdo_slot + block, :, head(h)]).astype(BF16)
-            dk = both(b.T, v_of(rows, h), q_of(rows, h), r.T)
-            dv = both(a.T, k_of(rows, h), do_of(rows, h), r)
-            ra[rows, head(h, k_col)] = dk
-            ra[rows, head(h, v_col)] = dv
+    group = 4
+
+    @pl.loop(0, n_heads)
+    def _(h):
+        @pl.when(due + h >= last_tick)
+        def _():
+            chain_step(0, h)
+
+        incoming = state_of(s_in, h)
+
+        @pl.loop(0, n_blocks // group)
+        def _(part):
+            for inner in range(group):
+                block = part * group + inner
+                rows = aligned(block, BLOCK_LEN)
+                a, b = scores(block, h)
+                s = (incoming + grads[kv_slot + block, :, head(h)]).astype(BF16)
+                xo[rows, head(h, dim)] = both(a, q_of(rows, h), v_of(rows, h), s)
+                ra[rows, head(h)] = both(b, do_of(rows, h), k_of(rows, h), s.T)
+
+    def rev_head(h):
+        incoming = state_of(r_in, h)
+
+        @pl.loop(0, n_blocks // group)
+        def _(part):
+            for inner in range(group):
+                block = part * group + inner
+                rows = aligned(block, BLOCK_LEN)
+                a, b = scores(block, h)
+                r = (incoming + grads[qdo_slot + block, :, head(h)]).astype(BF16)
+                dk = both(b.T, v_of(rows, h), q_of(rows, h), r.T)
+                dv = both(a.T, k_of(rows, h), do_of(rows, h), r)
+                ra[rows, head(h, k_col)] = dk
+                ra[rows, head(h, v_col)] = dv
 
     def credit(which):
         pl.semaphore_signal(credits.at[which], inc=1, device_id={"sp": previous}, device_id_type=MESH)
@@ -298,25 +323,20 @@
             def _():
                 pltpu.make_async_copy(grads.at[slot], red_out.at[late * early + piece], red_sems.at[late * early + piece]).start()
 
-    share = n_blocks // 4
+    gap = ((n_chips - 1) * early - n_heads) // (n_chips - 1)
+    rev_start = gap * (n_chips - 1 - chip)
 
     def reverse_work(index):
         @pl.when(index == 0)
         def _():
             accumulate(q_of, do_of, qdo_slot, r_out, True)
 
-        @pl.when(index == n_chips - chip)
-        def _():
-            for h in range(n_heads):
-                chain_step(1, h)
-
-        @pl.when((index > n_chips) & (index <= n_chips + 4))
-        def _():
-            @pl.loop(0, share)
-            def _(part):
-                rev_block((index - n_chips - 1) * share + part)
-
-        @pl.when(index == n_chips + 4)
+        @pl.when((index >= rev_start) & (index < rev_start + n_heads))
+        def _():
+            chain_step(1, index - rev_start)
+            rev_head(index - rev_start)
+
+        @pl.when(index == rev_start + n_heads - 1)
         def _():
             credit(1)
 
@@ -336,8 +356,8 @@
     for which, last in ((0, n_chips - 1), (1, 0)):
         @pl.when(chip != last)
         def _():
-            for h in range(n_heads):
-                chain_copy(which, h).wait_send()
+            for unit in range(n_heads * PARTS):
+                chain_copy(which, unit).wait_send()
 
     for late in range(2):
         @pl.loop(0, (n_chips - 1) * early)
@@ -502,7 +522,7 @@
         n_slots = 4 * (dim // TILE)
         pieces = n_slots // n_chips
         scale = 1.0 / math.sqrt(n_rows * n_seq * HEAD_DIM)
-        state = (n_heads, HEAD_DIM, HEAD_DIM)
+        state = (n_heads * PARTS, HEAD_DIM // PARTS, HEAD_DIM)
 
         red, own = pl.pallas_call(
             functools.partial(attention_kernel, n_seq, scale),
@@ -513,7 +533,7 @@
             + [pltpu.VMEM((rows, width), BF16)] * 2
             + [pltpu.VMEM((n_slots, TILE, width), F32), pltpu.VMEM((pieces, TILE, width), F32)]
             + [pltpu.VMEM(state, F32)] * 4
-            + [dma((2, 3)), dma((5,)), dma((2, 2, n_heads))]
+            + [dma((2, 3)), dma((5,)), dma((2, 2, n_heads * PARTS))]
             + [dma((2, n_chips - 1, pieces // 2))] * 2
             + [dma((4, 3)), dma((pieces,)), pltpu.SemaphoreType.REGULAR((2,))],
             compiler_params=params(0),

time: 452 us -> 462 us (1.022)
  Pallas kernels: 451 us -> 459 us
    pallas_call x1, Pallas kernels: 248 us -> 254 us  [local_layer(): pl.pallas_call(functools.partial(attention_kernel, n_seq, scale), out_sha...]
where the time goes in v5:
time: 462 us; the launch traced here: 460 us
  Pallas kernels  459 us (99%)
    pallas_call x1, Pallas kernels, local_layer(): pl.pallas_call(functools.partial(attention_kernel, n_seq, scale), out_sha...  254 us
    pallas_call x1, Pallas kernels, local_layer(): pl.pallas_call(functools.partial(gather_kernel, n_seq), out_shape=(pltpu....  191 us
    pallas_call x1, Pallas kernels, local_layer(): pl.pallas_call(place_kernel, out_shape=(jax.ShapeDtypeStruct((n_rows, dim...  14.1 us

profile of v5, /device:TPU:21, one launch (start us, length us, event | category | flops | bytes accessed | tf_op | source)
XLA Modules:
  0.0 460.0 jit_solution(16552934272765349033)
XLA Ops:
  0.6 254.1 %attention.1 = (f32[6,128,768]{2,1,0:T(8,128)}, bf16[4,1024,1536]{2,1,0:T(8,128)(2,1)}) custom-call(bf16[1024,1536]{1,0:T(8,128)(2,1)} %x.1, bf16[1024,1536]{1,0:T(8,128)(2,1)} %dy.1, bf16[1536,1536]{1,0:T(8,128)(2,1)} %wq.3, bf16[1536,1536]{1,0:T(8,128)(2,1)} %wk.3, bf16[1536,1536]{1,0:T(8,128)(2,1)} %wv.3, bf16[1536,1536]{1,0:T(8,128)(2,1)} %wo.3), custom_call_target="tpu_custom_call" | custom-call | tf_op jit(solution)/shard_map/attention/pallas_call | solution.py:527
  254.8 191.1 %gather.1 = (bf16[2,1024,1536]{2,1,0:T(8,128)(2,1)S(1)}, f32[2,48,128,768]{3,2,1,0:T(8,128)S(1)}) custom-call(f32[6,128,768]{2,1,0:T(8,128)} %get-tuple-element.10.red, bf16[4,1024,1536]{2,1,0:T(8,128)(2,1)} %get-tuple-element.11.own, bf16[1536,1536]{1,0:T(8,128)(2,1)} %wq.3, bf16[1536,1536]{1,0:T(8,128)(2,1)} %wk.3, bf16[1536,1536]{1,0:T(8,128)(2,1)} %wv.3, ...), custom_call_target="tpu_custom_call" | custom-call | tf_op jit(solution)/shard_map/gather/pallas_call | solution.py:546
  445.9 14.1 %place.1 = (bf16[1024,1536]{1,0:T(8,128)(2,1)}, bf16[1024,1536]{1,0:T(8,128)(2,1)}, f32[1536,1536]{1,0:T(8,128)}, f32[1536,1536]{1,0:T(8,128)}, f32[1536,1536]{1,0:T(8,128)}, /*index=5*/f32[1536,1536]{1,0:T(8,128)}) custom-call(bf16[2,1024,1536]{2,1,0:T(8,128)(2,1)S(1)} %get-tuple-element.12.results, f32[2,48,128,768]{3,2,1,0:T(8,128)S(1)} %get-tuple-element.13.both), custom_call_target="tpu_custom_call" | custom-call | tf_op jit(solution)/shard_map/place/pallas_call | solution.py:557

commit v6 on v2

--- a/solution.py
+++ b/solution.py
@@ -11,6 +11,7 @@
 BLOCK_LEN = 128
 TILE = 128
 ROWS = 256
+PROJECT_ROWS = 512
 MESH = pl.DeviceIdType.MESH
 VMEM_LIMIT = 67_043_328
 F32 = jnp.float32
@@ -97,11 +98,14 @@
     def weight(index, size):
         return w_s[pl.ds(index * size, size), :]
 
+    part_len = min(PROJECT_ROWS, n_rows)
+    steps = n_rows // part_len
+
     def part_rows(half, step):
-        return pl.ds(pl.multiple_of(half * n_rows + step * ROWS, ROWS), ROWS)
+        return pl.ds(pl.multiple_of(half * n_rows + step * part_len, part_len), part_len)
 
     def project_kv(half):
-        @pl.loop(0, n_rows // ROWS)
+        @pl.loop(0, steps)
         def _(step):
             rows = part_rows(half, step)
             ra[rows, pl.ds(k_col, width)] = dot(xo[rows, x_part], weight(0, dim)).astype(BF16)
@@ -120,14 +124,15 @@
     def accumulate(left, right, slot, total, reverse):
         total[...] = jnp.zeros_like(total)
 
-        @pl.loop(0, n_blocks)
+        @pl.loop(0, n_blocks // 2)
         def _(step):
-            block = (n_blocks - 1 - step) if reverse else step
-            rows = aligned(block, BLOCK_LEN)
-            for h in range(n_heads):
-                running = total[h]
-                grads[slot + block, :, head(h)] = running
-                total[h] = running + dot_t(left(rows, h), right(rows, h))
+            for inner in range(2):
+                block = (n_blocks - 1 - 2 * step - inner) if reverse else 2 * step + inner
+                rows = aligned(block, BLOCK_LEN)
+                for h in range(n_heads):
+                    running = total[h]
+                    grads[slot + block, :, head(h)] = running
+                    total[h] = running + dot_t(left(rows, h), right(rows, h))
 
     def q_of(rows, h):
         return q[rows, head(h)]
@@ -169,12 +174,11 @@
 
     accumulate(k_of, v_of, kv_slot, s_out, False)
 
-    steps = n_rows // ROWS
-
     def project_qdo(half, first_tick):
         @pl.loop(0, steps)
         def _(step):
-            chain_s(first_tick + step)
+            chain_s(first_tick + 2 * step)
+            chain_s(first_tick + 2 * step + 1)
             rows = part_rows(half, step)
             q[rows, :] = dot(xo[rows, x_part], weight(2, dim)).astype(BF16)
             product = dot_nt(ra[rows, pl.ds(width, width)], weight(6, width))
@@ -185,7 +189,7 @@
         load.wait()
     project_qdo(core, 0)
     remote[1].wait()
-    project_qdo(1 - core, steps)
+    project_qdo(1 - core, 2 * steps)
 
     causal = lax.broadcasted_iota(jnp.int32, (BLOCK_LEN, BLOCK_LEN), 0) >= lax.broadcasted_iota(jnp.int32, (BLOCK_LEN, BLOCK_LEN), 1)
 
@@ -197,13 +201,14 @@
             w_s[a_rows, head(h)] = jnp.where(causal, dot_nt(q_of(rows, h), k_of(rows, h)), 0.0).astype(BF16)
             w_s[b_rows, head(h)] = jnp.where(causal, dot_nt(do_of(rows, h), v_of(rows, h)), 0.0).astype(BF16)
 
-    @pl.loop(0, max(3 * (n_chips - 1) + n_heads - 2 * steps, n_blocks))
+    @pl.loop(0, max(3 * (n_chips - 1) + n_heads - 4 * steps, n_blocks // 2))
     def _(step):
-        chain_s(2 * steps + step)
-
-        @pl.when(step < n_blocks)
-        def _():
-            block_scores(step)
+        chain_s(4 * steps + step)
+
+        @pl.when(step < n_blocks // 2)
+        def _():
+            for inner in range(2):
+                block_scores(2 * step + inner)
 
     def scores(block, h):
         a_rows = pl.ds(pl.multiple_of(a_row + block * BLOCK_LEN, BLOCK_LEN), BLOCK_LEN)
@@ -214,14 +219,16 @@
         out = dot(jnp.concatenate([left, right], axis=1), jnp.concatenate([top, bottom], axis=0))
         return (out * scale).astype(BF16)
 
-    @pl.loop(0, n_blocks)
-    def _(block):
-        rows = aligned(block, BLOCK_LEN)
-        for h in range(n_heads):
-            a, b = scores(block, h)
-            s = (s_in[h] + grads[kv_slot + block, :, head(h)]).astype(BF16)
-            xo[rows, head(h, dim)] = both(a, q_of(rows, h), v_of(rows, h), s)
-            ra[rows, head(h)] = both(b, do_of(rows, h), k_of(rows, h), s.T)
+    @pl.loop(0, n_blocks // 2)
+    def _(step):
+        for inner in range(2):
+            block = 2 * step + inner
+            rows = aligned(block, BLOCK_LEN)
+            for h in range(n_heads):
+                a, b = scores(block, h)
+                s = (s_in[h] + grads[kv_slot + block, :, head(h)]).astype(BF16)
+                xo[rows, head(h, dim)] = both(a, q_of(rows, h), v_of(rows, h), s)
+                ra[rows, head(h)] = both(b, do_of(rows, h), k_of(rows, h), s.T)
 
     def rev_block(block):
         rows = aligned(block, BLOCK_LEN)

time: 452 us -> 449 us (level)
  no operation moved by 1% of the time
where the time goes in v6:
time: 449 us; the launch traced here: 448 us
  Pallas kernels  447 us (100%)
    pallas_call x1, Pallas kernels, local_layer(): pl.pallas_call(functools.partial(attention_kernel, n_seq, scale), out_sha...  244 us
    pallas_call x1, Pallas kernels, local_layer(): pl.pallas_call(functools.partial(gather_kernel, n_seq), out_shape=(pltpu....  189 us
    pallas_call x1, Pallas kernels, local_layer(): pl.pallas_call(place_kernel, out_shape=(jax.ShapeDtypeStruct((n_rows, dim...  14.1 us

profile of v6, /device:TPU:21, one launch (start us, length us, event | category | flops | bytes accessed | tf_op | source)
XLA Modules:
  0.0 447.9 jit_solution(14491896037696859789)
XLA Ops:
  0.6 244.5 %attention.1 = (f32[6,128,768]{2,1,0:T(8,128)}, bf16[4,1024,1536]{2,1,0:T(8,128)(2,1)}) custom-call(bf16[1024,1536]{1,0:T(8,128)(2,1)} %x.1, bf16[1024,1536]{1,0:T(8,128)(2,1)} %dy.1, bf16[1536,1536]{1,0:T(8,128)(2,1)} %wq.3, bf16[1536,1536]{1,0:T(8,128)(2,1)} %wk.3, bf16[1536,1536]{1,0:T(8,128)(2,1)} %wv.3, bf16[1536,1536]{1,0:T(8,128)(2,1)} %wo.3), custom_call_target="tpu_custom_call" | custom-call | tf_op jit(solution)/shard_map/attention/pallas_call | solution.py:514
  245.1 188.7 %gather.1 = (bf16[2,1024,1536]{2,1,0:T(8,128)(2,1)S(1)}, f32[2,48,128,768]{3,2,1,0:T(8,128)S(1)}) custom-call(f32[6,128,768]{2,1,0:T(8,128)} %get-tuple-element.10.red, bf16[4,1024,1536]{2,1,0:T(8,128)(2,1)} %get-tuple-element.11.own, bf16[1536,1536]{1,0:T(8,128)(2,1)} %wq.3, bf16[1536,1536]{1,0:T(8,128)(2,1)} %wk.3, bf16[1536,1536]{1,0:T(8,128)(2,1)} %wv.3, ...), custom_call_target="tpu_custom_call" | custom-call | tf_op jit(solution)/shard_map/gather/pallas_call | solution.py:533
  433.9 14.1 %place.1 = (bf16[1024,1536]{1,0:T(8,128)(2,1)}, bf16[1024,1536]{1,0:T(8,128)(2,1)}, f32[1536,1536]{1,0:T(8,128)}, f32[1536,1536]{1,0:T(8,128)}, f32[1536,1536]{1,0:T(8,128)}, /*index=5*/f32[1536,1536]{1,0:T(8,128)}) custom-call(bf16[2,1024,1536]{2,1,0:T(8,128)(2,1)S(1)} %get-tuple-element.12.results, f32[2,48,128,768]{3,2,1,0:T(8,128)S(1)} %get-tuple-element.13.both), custom_call_target="tpu_custom_call" | custom-call | tf_op jit(solution)/shard_map/place/pallas_call | solution.py:544

commit v7 on v6

--- a/solution.py
+++ b/solution.py
@@ -77,23 +77,24 @@
     k_col, v_col, a_row, b_row = width + dim, 2 * width + dim, 0, all_rows
     kv_slot, qdo_slot = 0, n_slots // 2
 
-    entry_barrier((peer, up, down))
     x_part, dy_part = pl.ds(0, dim), pl.ds(width, dim)
     local, remote = [], []
     for index, (src, dst) in enumerate(((x, xo.at[own_rows, x_part]), (dy, ra.at[own_rows, dy_part]))):
-        remote.append(send(src, dst, x_sems.at[index, 0], x_sems.at[index, 1], peer))
         local.append(pltpu.make_async_copy(src, dst, x_sems.at[index, 2]))
+        remote.append(send(dst, dst, x_sems.at[index, 0], x_sems.at[index, 1], peer))
     w_loads = [pltpu.make_async_copy(weight.at[:, w_cols], w_s.at[pl.ds(index * dim, dim)], w_sems.at[index]) for index, weight in enumerate((wk, wv, wq))]
     for part in range(2):
         w_loads.append(pltpu.make_async_copy(wo.at[w_cols, pl.ds(part * width, width)], w_s.at[pl.ds(3 * dim + part * width, width)], w_sems.at[3 + part]))
-    remote[0].start()
     local[0].start()
     for load in w_loads[:2]:
         load.start()
-    remote[1].start()
+    local[1].start()
     for load in w_loads[2:]:
         load.start()
-    local[1].start()
+    entry_barrier((peer, up, down))
+    for index in range(2):
+        local[index].wait()
+        remote[index].start()
 
     def weight(index, size):
         return w_s[pl.ds(index * size, size), :]
@@ -111,7 +112,6 @@
             ra[rows, pl.ds(k_col, width)] = dot(xo[rows, x_part], weight(0, dim)).astype(BF16)
             ra[rows, pl.ds(v_col, width)] = dot(xo[rows, x_part], weight(1, dim)).astype(BF16)
 
-    local[0].wait()
     w_loads[0].wait()
     w_loads[1].wait()
     project_kv(core)
@@ -185,7 +185,7 @@
             product += dot_nt(ra[rows, pl.ds(2 * width, width)], weight(7, width))
             do[rows, :] = product.astype(BF16)
 
-    for load in w_loads[2:] + [local[1]]:
+    for load in w_loads[2:]:
         load.wait()
     project_qdo(core, 0)
     remote[1].wait()

time: 449 us -> 447 us (level)
  no operation moved by 1% of the time
where the time goes in v7:
time: 447 us; the launch traced here: 446 us
  Pallas kernels  446 us (100%)
    pallas_call x1, Pallas kernels, local_layer(): pl.pallas_call(functools.partial(attention_kernel, n_seq, scale), out_sha...  242 us
    pallas_call x1, Pallas kernels, local_layer(): pl.pallas_call(functools.partial(gather_kernel, n_seq), out_shape=(pltpu....  189 us
    pallas_call x1, Pallas kernels, local_layer(): pl.pallas_call(place_kernel, out_shape=(jax.ShapeDtypeStruct((n_rows, dim...  14.1 us

profile of v7, /device:TPU:21, one launch (start us, length us, event | category | flops | bytes accessed | tf_op | source)
XLA Modules:
  0.0 446.3 jit_solution(5646020037215231311)
XLA Ops:
  0.6 242.3 %attention.1 = (f32[6,128,768]{2,1,0:T(8,128)}, bf16[4,1024,1536]{2,1,0:T(8,128)(2,1)}) custom-call(bf16[1024,1536]{1,0:T(8,128)(2,1)} %x.1, bf16[1024,1536]{1,0:T(8,128)(2,1)} %dy.1, bf16[1536,1536]{1,0:T(8,128)(2,1)} %wq.3, bf16[1536,1536]{1,0:T(8,128)(2,1)} %wk.3, bf16[1536,1536]{1,0:T(8,128)(2,1)} %wv.3, bf16[1536,1536]{1,0:T(8,128)(2,1)} %wo.3), custom_call_target="tpu_custom_call" | custom-call | tf_op jit(solution)/shard_map/attention/pallas_call | solution.py:514
  243.0 189.3 %gather.1 = (bf16[2,1024,1536]{2,1,0:T(8,128)(2,1)S(1)}, f32[2,48,128,768]{3,2,1,0:T(8,128)S(1)}) custom-call(f32[6,128,768]{2,1,0:T(8,128)} %get-tuple-element.10.red, bf16[4,1024,1536]{2,1,0:T(8,128)(2,1)} %get-tuple-element.11.own, bf16[1536,1536]{1,0:T(8,128)(2,1)} %wq.3, bf16[1536,1536]{1,0:T(8,128)(2,1)} %wk.3, bf16[1536,1536]{1,0:T(8,128)(2,1)} %wv.3, ...), custom_call_target="tpu_custom_call" | custom-call | tf_op jit(solution)/shard_map/gather/pallas_call | solution.py:533
  432.2 14.1 %place.1 = (bf16[1024,1536]{1,0:T(8,128)(2,1)}, bf16[1024,1536]{1,0:T(8,128)(2,1)}, f32[1536,1536]{1,0:T(8,128)}, f32[1536,1536]{1,0:T(8,128)}, f32[1536,1536]{1,0:T(8,128)}, /*index=5*/f32[1536,1536]{1,0:T(8,128)}) custom-call(bf16[2,1024,1536]{2,1,0:T(8,128)(2,1)S(1)} %get-tuple-element.12.results, f32[2,48,128,768]{3,2,1,0:T(8,128)S(1)} %get-tuple-element.13.both), custom_call_target="tpu_custom_call" | custom-call | tf_op jit(solution)/shard_map/place/pallas_call | solution.py:544

commit v8 on v7

--- a/solution.py
+++ b/solution.py
@@ -264,14 +264,15 @@
         slot, sems = hop(late, step, piece)
         send(slot, land.at[late * early + piece] if first else slot, *sems, following).start()
 
-    def run_ring(late, extra):
-        offset = late * (n_slots // 2)
-
+    def start_ring(late):
         @pl.loop(0, early)
         def _(piece):
             unit = unit_of(0, piece)
-            grads[offset + unit] = term(late, unit)
+            grads[late * (n_slots // 2) + unit] = term(late, unit)
             start_hop(late, 0, piece, True)
+
+    def run_ring(late, extra):
+        offset = late * (n_slots // 2)
 
         @pl.loop(0, (n_chips - 1) * early)
         def _(index):
@@ -327,7 +328,12 @@
         def _():
             credit(1)
 
+        @pl.when(index == (n_chips - 2) * early)
+        def _():
+            start_ring(1)
+
     credit(0)
+    start_ring(0)
     run_ring(0, reverse_work)
 
     copies = []

time: 447 us -> 445 us (level)
  no operation moved by 1% of the time
where the time goes in v8:
time: 445 us; the launch traced here: 444 us
  Pallas kernels  444 us (100%)
    pallas_call x1, Pallas kernels, local_layer(): pl.pallas_call(functools.partial(attention_kernel, n_seq, scale), out_sha...  239 us
    pallas_call x1, Pallas kernels, local_layer(): pl.pallas_call(functools.partial(gather_kernel, n_seq), out_shape=(pltpu....  191 us
    pallas_call x1, Pallas kernels, local_layer(): pl.pallas_call(place_kernel, out_shape=(jax.ShapeDtypeStruct((n_rows, dim...  14.1 us

profile of v8, /device:TPU:21, one launch (start us, length us, event | category | flops | bytes accessed | tf_op | source)
XLA Modules:
  0.0 444.4 jit_solution(17657518547441734807)
XLA Ops:
  0.6 239.0 %attention.1 = (f32[6,128,768]{2,1,0:T(8,128)}, bf16[4,1024,1536]{2,1,0:T(8,128)(2,1)}) custom-call(bf16[1024,1536]{1,0:T(8,128)(2,1)} %x.1, bf16[1024,1536]{1,0:T(8,128)(2,1)} %dy.1, bf16[1536,1536]{1,0:T(8,128)(2,1)} %wq.3, bf16[1536,1536]{1,0:T(8,128)(2,1)} %wk.3, bf16[1536,1536]{1,0:T(8,128)(2,1)} %wv.3, bf16[1536,1536]{1,0:T(8,128)(2,1)} %wo.3), custom_call_target="tpu_custom_call" | custom-call | tf_op jit(solution)/shard_map/attention/pallas_call | solution.py:520
  239.7 190.6 %gather.1 = (bf16[2,1024,1536]{2,1,0:T(8,128)(2,1)S(1)}, f32[2,48,128,768]{3,2,1,0:T(8,128)S(1)}) custom-call(f32[6,128,768]{2,1,0:T(8,128)} %get-tuple-element.10.red, bf16[4,1024,1536]{2,1,0:T(8,128)(2,1)} %get-tuple-element.11.own, bf16[1536,1536]{1,0:T(8,128)(2,1)} %wq.3, bf16[1536,1536]{1,0:T(8,128)(2,1)} %wk.3, bf16[1536,1536]{1,0:T(8,128)(2,1)} %wv.3, ...), custom_call_target="tpu_custom_call" | custom-call | tf_op jit(solution)/shard_map/gather/pallas_call | solution.py:539
  430.3 14.1 %place.1 = (bf16[1024,1536]{1,0:T(8,128)(2,1)}, bf16[1024,1536]{1,0:T(8,128)(2,1)}, f32[1536,1536]{1,0:T(8,128)}, f32[1536,1536]{1,0:T(8,128)}, f32[1536,1536]{1,0:T(8,128)}, /*index=5*/f32[1536,1536]{1,0:T(8,128)}) custom-call(bf16[2,1024,1536]{2,1,0:T(8,128)(2,1)S(1)} %get-tuple-element.12.results, f32[2,48,128,768]{3,2,1,0:T(8,128)S(1)} %get-tuple-element.13.both), custom_call_target="tpu_custom_call" | custom-call | tf_op jit(solution)/shard_map/place/pallas_call | solution.py:550
